TPU v7x, 128 devices: a whole 4x4x4 slice. The times are simulated.
128 devices in a mesh: seq: 32 (over x, z, core), tp: 4 (over y).
Axes of the slice: x: 4, y: 4, z: 4, core: 2. Of those that a mesh axis runs over, the one named last changes fastest.
Arguments:
- tokens: bfloat16 [65536, 2560], P('seq'), may hold values from -6 to 6
- w_query: bfloat16 [2560, 512], P(None, 'tp'), may hold values from -0.009765625 to 0.009765625
- w_key: bfloat16 [2560, 512], P(None, 'tp'), may hold values from -0.00048828125 to 0.00048828125
- w_value: bfloat16 [2560, 1024], P(None, 'tp'), may hold values from -0.125 to 0.125
- w_gate: bfloat16 [2560, 512], P(None, 'tp'), may hold values from -0.125 to 0.125
- gate_rate: float32 [512], P('tp'), may hold values from 3.8146973e-06 to 3.0517578e-05
- out_grad: bfloat16 [65536, 1024], P('seq', 'tp'), may hold values from -6 to 6
Outputs:
- input_grad: bfloat16 [65536, 2560], P(('seq', 'tp'))
- gate_signal: float32 [65536, 512], P('seq', 'tp')
All inputs are finite; a program needn't handle non-finite values.
Results may differ from a plain program's by a relative error of at most 0.015.
Values sent between devices are 32-bit elements.
A program may use at most 192 MiB of HBM per device.

v0:
```python
import functools
import math

import jax
import jax.numpy as jnp
from jax import lax
from jax.experimental import pallas as pl
from jax.experimental.pallas import tpu as pltpu
from jax.sharding import PartitionSpec as P

CH = 128
PAD = 8
VMEM_LIMIT = 66 * 1000 * 1000
F32, BF16 = jnp.float32, jnp.bfloat16


def mm(left, right, dims):
    return lax.dot_general(left, right, (dims, ((), ())), preferred_element_type=F32)


NN = ((1,), (0,))
NT = ((1,), (1,))
TN = ((0,), (0,))


def tri_sum(triangle, rows):
    high = rows.astype(BF16)
    low = (rows - high.astype(F32)).astype(BF16)
    return mm(triangle, high, NN) + mm(triangle, low, NN)


def kernel(
    seq, tp, dk, dv, tile, scale,
    tok, wq, wk, wv, wg, rate_ref, dout_ref,
    grad_ref, sig_ref,
    wcat, xbuf, proj, sq_all, w_all, s_all, m_all, cl_all, msg, got, edge,
    wout0, wout1, wout2, wout3, land0, land1, land2, land3, wfar, g_own, g_send, g_recv, part_own, part_send, part_recv,
    w_sem, x_sem, msg_send, msg_recv, gs_sem, gr_sem, ps_sem, pr_sem, first_sem, ring_s, ring_r,
):
    me, rank = lax.axis_index("seq"), lax.axis_index("tp")
    length, width = dout_ref.shape[0], wcat.shape[0]
    blocks, tiles = length // CH, length // tile
    each = blocks // tp
    half = each // 2
    core = rank + 1 - 2 * lax.rem(rank, 2)
    far = lax.rem(rank + 2, 4)
    far_core = lax.rem(core + 2, 4)
    half_ring, row = seq // 2, me // 2
    place = row + lax.rem(me, 2) * (seq - 1 - 2 * row)
    depth = width // seq

    def seq_at(p):
        p = lax.rem(p + seq, seq)
        return 2 * p + (p // half_ring) * (2 * seq - 1 - 4 * p)

    onward = (seq_at(place + 1), seq_at(place - 1))
    wouts, lands = (wout0, wout1, wout2, wout3), (land0, land1, land2, land3)
    starts = [sum(w.shape[0] for w in wouts[:n]) for n in range(4)]

    def cross(way):
        return pltpu.make_async_remote_copy(
            src_ref=wouts[way], dst_ref=lands[way].at[0], send_sem=first_sem.at[way],
            recv_sem=ring_r.at[way, 0], device_id={"tp": far},
            device_id_type=pl.DeviceIdType.MESH,
        )

    def ring(way, k):
        return pltpu.make_async_remote_copy(
            src_ref=lands[way].at[k], dst_ref=lands[way].at[k + 1], send_sem=ring_s.at[way, k],
            recv_sem=ring_r.at[way, k + 1], device_id={"seq": onward[way % 2]},
            device_id_type=pl.DeviceIdType.MESH,
        )

    def pump(k, part):
        for way in (2 * part, 2 * part + 1):
            if isinstance(k, int) and k == 0:
                cross(way).wait_recv()
            else:
                ring(way, k - 1).wait_recv()
            ring(way, k).start()

    def x_copy(t, slot):
        return pltpu.make_async_copy(
            tok.at[pl.ds(pl.multiple_of(t * tile, tile), tile), :], xbuf.at[slot], x_sem.at[slot]
        )

    loads = []
    for n, (w, start, size) in enumerate(
        ((wq, 0, dk), (wk, dk, dk), (wv, 2 * dk, dv), (wg, 2 * dk + dv, dk))
    ):
        loads.append(pltpu.make_async_copy(w, wcat.at[:, pl.ds(start, size)], w_sem.at[n]))
    x_copy(0, 0).start()
    for load in loads:
        load.start()

    barrier = pltpu.get_barrier_semaphore()
    for d in range(1, seq):
        pl.semaphore_signal(
            barrier, inc=1, device_id={"seq": lax.rem(me + d, seq)},
            device_id_type=pl.DeviceIdType.MESH,
        )
    for other in (core, far):
        pl.semaphore_signal(
            barrier, inc=1, device_id={"tp": other}, device_id_type=pl.DeviceIdType.MESH
        )

    rows_at = lax.broadcasted_iota(jnp.int32, (CH, CH), 0)
    cols_at = lax.broadcasted_iota(jnp.int32, (CH, CH), 1)
    lower = (rows_at >= cols_at).astype(F32)
    lower_b = lower.astype(BF16)
    upper_b = (rows_at <= cols_at).astype(BF16)
    rate = rate_ref[...]

    zero_state = jnp.zeros((dv, dk), F32)
    msg[0, pl.ds(0, dv), :] = zero_state
    msg[1, pl.ds(0, dv), :] = zero_state
    for load in loads:
        load.wait()
    for way in range(4):
        size = wouts[way].shape[0]
        at = pl.multiple_of(me * depth + starts[way], 16)
        wouts[way][...] = wcat[pl.ds(at, size), :].astype(F32)
    pl.semaphore_wait(barrier, seq + 1)
    for way in range(4):
        cross(way).start()

    def project(t, total):
        slot = lax.rem(t, 2)

        @pl.when(t + 1 < tiles)
        def _():
            x_copy(t + 1, 1 - slot).start()

        @pl.when(t == tiles - 2)
        def _():
            pump(0, 0)

        x_copy(t, slot).wait()
        out = mm(xbuf[slot], wcat[...], NN)
        base = pl.multiple_of(t * tile, tile)
        proj[pl.ds(base, tile), :] = out[:, : 2 * dk + dv].astype(BF16)
        squashed = jax.nn.sigmoid(out[:, 2 * dk + dv :])
        sq_all[pl.ds(base, tile), :] = squashed
        for j in range(tile // CH):
            part = slice(j * CH, (j + 1) * CH)
            b = t * (tile // CH) + j
            within = tri_sum(lower_b, -rate * squashed[part])
            w_all[pl.ds(pl.multiple_of(base + j * CH, CH), CH), :] = within
            closing = within[CH - 1 : CH]
            cl_all[b] = jnp.broadcast_to(closing, (PAD, dk))
            query = out[part, :dk].astype(BF16).astype(F32)
            key = out[part, dk : 2 * dk].astype(BF16).astype(F32)
            value = out[part, 2 * dk : 2 * dk + dv].astype(BF16)
            dout = dout_ref[pl.ds(pl.multiple_of(base + j * CH, CH), CH), :]
            query_scaled = (query * jnp.exp(within)).astype(BF16)
            key_closing = (key * jnp.exp(closing - within)).astype(BF16)
            state = msg[0, pl.ds(0, dv), :]
            s_all[b] = state
            msg[0, pl.ds(0, dv), :] = jnp.exp(closing) * state + mm(value, key_closing, TN)
            fed = mm(dout, query_scaled, TN)
            m_all[b] = fed
            msg[1, pl.ds(0, dv), :] += jnp.exp(total) * fed
            total = total + closing
        return total

    total = lax.fori_loop(0, tiles, project, jnp.zeros((1, dk), F32))
    decay = jnp.broadcast_to(jnp.exp(total), (PAD, dk))
    msg[0, pl.ds(dv, PAD), :] = decay
    msg[1, pl.ds(dv, PAD), :] = decay

    def exchange(d):
        return pltpu.make_async_remote_copy(
            src_ref=msg.at[(me + d) // seq],
            dst_ref=got.at[d],
            send_sem=msg_send.at[d],
            recv_sem=msg_recv.at[d],
            device_id={"seq": lax.rem(me + d, seq)},
            device_id_type=pl.DeviceIdType.MESH,
        )

    def start_exchange(d, carry):
        exchange(d).start()
        return carry

    def wait_exchange(d, carry):
        exchange(d).wait()
        return carry

    lax.fori_loop(1, seq, start_exchange, 0)
    pump(0, 1)
    lax.fori_loop(1, seq, wait_exchange, 0)
    pump(1, 0)

    edge[...] = jnp.zeros_like(edge)

    def fold(which, d):
        edge[which] = got[d, pl.ds(dv, 1), :] * edge[which] + got[d, pl.ds(0, dv), :]

    def fold_states(j, carry):
        fold(0, me - j)
        return carry

    def fold_grads(d, carry):
        fold(1, d)
        return carry

    lax.fori_loop(0, me, fold_states, 0)
    lax.fori_loop(me + 1, seq, fold_grads, 0)

    def enter(b, so_far):
        s_all[b] = s_all[b] + jnp.exp(so_far) * edge[0]
        return so_far + cl_all[b, 0:1, :]

    lax.fori_loop(0, blocks, enter, jnp.zeros((1, dk), F32))

    def leave(j, carry):
        b = blocks - 1 - j
        fed = m_all[b]
        leaving = edge[1]
        m_all[b] = leaving
        edge[1] = jnp.exp(cl_all[b, 0:1, :]) * leaving + fed
        return carry

    lax.fori_loop(0, blocks, leave, 0)

    def grads(b):
        rows = pl.ds(pl.multiple_of(b * CH, CH), CH)
        query = proj[rows, 0:dk].astype(F32)
        key = proj[rows, dk : 2 * dk].astype(F32)
        value = proj[rows, 2 * dk : 2 * dk + dv]
        within, squashed, dout = w_all[rows, :], sq_all[rows, :], dout_ref[rows, :]
        closing = within[CH - 1 : CH]
        state, leaving = s_all[b], m_all[b]
        grow, shrink, rest = jnp.exp(within), jnp.exp(-within), jnp.exp(closing - within)
        query_f, key_f, close_f = query * grow, key * shrink, key * rest
        query_s, key_s, close_s = query_f.astype(BF16), key_f.astype(BF16), close_f.astype(BF16)
        scores = (mm(query_s, key_s, NT) * lower).astype(BF16)
        d_scores = (mm(dout, value, NT) * lower).astype(BF16)
        leaving_b = leaving.astype(BF16)
        d_query_s = mm(dout, state.astype(BF16), NN) + mm(d_scores, key_s, NN)
        d_key_s = mm(d_scores, query_s, TN)
        d_close = mm(value, leaving_b, NN)
        d_value = mm(scores, dout, TN) + mm(close_s, leaving_b, NT)
        d_query = d_query_s * grow
        d_key = d_key_s * shrink + d_close * rest
        at_close = d_close * close_f
        d_within = d_query_s * query_f - d_key_s * key_f - at_close
        d_closing = jnp.sum(at_close, axis=0, keepdims=True) + jnp.exp(closing) * jnp.sum(
            leaving * state, axis=0, keepdims=True
        )
        d_gate = tri_sum(upper_b, d_within) + d_closing
        pre = d_gate * -rate * squashed * (1.0 - squashed)
        sig_ref[rows, :] = pre * scale
        return d_query, d_key, d_value, pre

    bounds = ((0, dk), (dk, 2 * dk), (2 * dk, 2 * dk + dv), (2 * dk + dv, 3 * dk + dv))
    step = 512 if width % 512 == 0 else width

    def spread(packed, weight, put):
        for at in range(0, width, step):
            cols = slice(at, at + step)
            put(cols, mm(packed, weight[cols, :], NT))

    def copy_g(i):
        return pltpu.make_async_remote_copy(
            src_ref=g_send.at[i], dst_ref=g_recv.at[i], send_sem=gs_sem.at[i],
            recv_sem=gr_sem.at[i], device_id={"tp": far}, device_id_type=pl.DeviceIdType.MESH,
        )

    def copy_p(i):
        return pltpu.make_async_remote_copy(
            src_ref=part_send.at[i], dst_ref=part_recv.at[i], send_sem=ps_sem.at[i],
            recv_sem=pr_sem.at[i], device_id={"tp": core}, device_id_type=pl.DeviceIdType.MESH,
        )

    steps = iter([(k, part) for k in range(1, seq - 1) for part in (0, 1)][1:])

    def pump_next():
        k = next(steps, None)
        if k is not None:
            pump(*k)

    def away(chunk, base):
        def run(i, carry):
            for (lo, hi), part in zip(bounds, grads(chunk * each + i)):
                g_send[base + i, :, lo:hi] = part
            copy_g(base + i).start()
            return carry

        lax.fori_loop(0, half, run, 0)
        pump_next()
        lax.fori_loop(half, each, run, 0)
        pump_next()

    def home(chunk, base):
        def run(i, carry):
            for (lo, hi), part in zip(bounds, grads(chunk * each + i)):
                g_own[base + i, :, lo:hi] = part.astype(BF16)
            return carry

        lax.fori_loop(0, half, run, 0)
        pump_next()
        lax.fori_loop(half, each, run, 0)
        pump_next()

    def rows_of(buffer, i):
        return jnp.concatenate([buffer[2 * i], buffer[2 * i + 1]], axis=0).astype(BF16)

    away(far_core, 0)
    away(far, each)
    home(core, 0)
    home(rank, each)

    def own_part(i, carry):
        def put_send(cols, part):
            part_send[i, :, cols] = part

        def put_own(cols, part):
            part_own[i, :, cols] = part

        spread(rows_of(g_own, i), wcat, put_send)
        spread(rows_of(g_own, half + i), wcat, put_own)
        return carry

    lax.fori_loop(0, half, own_part, 0)
    done, part = next(steps, (seq - 1, 0))
    if part == 1:
        pump(done, 1)
        done += 1

    def pump_rest(k, carry):
        pump(k, 0)
        pump(k, 1)
        return carry

    lax.fori_loop(done, seq - 1, pump_rest, 0)
    def unpack(k, carry):
        for way in range(4):
            origin = seq_at(place + k) if way % 2 else seq_at(place - k)
            size = wouts[way].shape[0]
            at = pl.multiple_of(origin * depth + starts[way], 16)
            wfar[pl.ds(at, size), :] = lands[way][k].astype(BF16)
        return carry

    lax.fori_loop(0, seq - 1, unpack, 0)
    for way in range(4):
        ring(way, seq - 2).wait_recv()
    unpack(seq - 1, 0)

    def send_part(i, carry):
        copy_g(2 * i).wait()
        copy_g(2 * i + 1).wait()

        def put(cols, part):
            part_send[i, :, cols] = part_send[i, :, cols] + part

        spread(rows_of(g_recv, i), wfar, put)
        copy_p(i).start()
        return carry

    lax.fori_loop(0, half, send_part, 0)

    def finish(i, carry):
        copy_g(2 * (half + i)).wait()
        copy_g(2 * (half + i) + 1).wait()
        copy_p(i).wait()
        rows = pl.ds(pl.multiple_of(i * 2 * CH, 2 * CH), 2 * CH)

        def put(cols, part):
            grad_ref[rows, cols] = (
                part_own[i, :, cols] + part + part_recv[i, :, cols]
            ).astype(BF16)

        spread(rows_of(g_recv, half + i), wfar, put)
        return carry

    lax.fori_loop(0, half, finish, 0)

    def drain(k, carry):
        for way in range(4):
            ring(way, k).wait_send()
        return carry

    for way in range(4):
        cross(way).wait_send()
    lax.fori_loop(0, seq - 1, drain, 0)


def solution(mesh):
    seq, tp = mesh.shape["seq"], mesh.shape["tp"]

    def body(tokens, w_query, w_key, w_value, w_gate, gate_rate, out_grad):
        length, width = tokens.shape
        dk, dv = w_query.shape[1], w_value.shape[1]
        blocks, each = length // CH, length // CH // tp
        tile = 2 * CH
        scale = 4.0 * math.sqrt(length * seq * dk / dv)
        depth = width // seq
        units = depth // 16
        sizes = [16 * ((units + 3 - n) // 4) for n in range(4)]
        hbm = pl.BlockSpec(memory_space=pl.ANY)
        vmem = pl.BlockSpec(memory_space=pltpu.VMEM)
        dma = pltpu.SemaphoreType.DMA
        return pl.pallas_call(
            functools.partial(kernel, seq, tp, dk, dv, tile, scale),
            out_shape=(
                jax.ShapeDtypeStruct((length // tp, width), BF16),
                jax.ShapeDtypeStruct((length, dk), F32),
            ),
            in_specs=[hbm] * 5 + [vmem] * 2,
            out_specs=(vmem, vmem),
            scratch_shapes=[
                pltpu.VMEM((width, 3 * dk + dv), BF16),
                pltpu.VMEM((2, tile, width), BF16),
                pltpu.VMEM((length, 2 * dk + dv), BF16),
                pltpu.VMEM((length, dk), F32),
                pltpu.VMEM((length, dk), F32),
                pltpu.VMEM((blocks, dv, dk), F32),
                pltpu.VMEM((blocks, dv, dk), F32),
                pltpu.VMEM((blocks, PAD, dk), F32),
                pltpu.VMEM((2, dv + PAD, dk), F32),
                pltpu.VMEM((seq, dv + PAD, dk), F32),
                pltpu.VMEM((2, dv, dk), F32),
            ]
            + [pltpu.VMEM((size, 3 * dk + dv), F32) for size in sizes]
            + [pltpu.VMEM((seq, size, 3 * dk + dv), F32) for size in sizes]
            + [pltpu.VMEM((width, 3 * dk + dv), BF16)]
            + [pltpu.VMEM((2 * each, CH, 3 * dk + dv), kind) for kind in (BF16, F32, F32)]
            + [pltpu.VMEM((each // 2, 2 * CH, width), F32)] * 3
            + [dma((4,)), dma((2,)), dma((seq,)), dma((seq,))]
            + [dma((2 * each,))] * 2
            + [dma((each // 2,))] * 2
            + [dma((4,)), dma((4, seq)), dma((4, seq))],
            compiler_params=pltpu.CompilerParams(
                collective_id=0, has_side_effects=True, vmem_limit_bytes=VMEM_LIMIT
            ),
        )(tokens, w_query, w_key, w_value, w_gate, gate_rate.reshape(1, dk), out_grad)

    placed = (
        P("seq", None),
        P(None, "tp"),
        P(None, "tp"),
        P(None, "tp"),
        P(None, "tp"),
        P("tp"),
        P("seq", "tp"),
    )
    return jax.shard_map(
        body,
        mesh=mesh,
        in_specs=placed,
        out_specs=(P(("seq", "tp"), None), P("seq", "tp")),
        check_vma=False,
    )
```

profile of v0, /device:TPU:1, one launch (start us, length us, event | category | flops | bytes accessed | tf_op | source)
XLA Modules:
  0.0 348.0 jit_solution(13982549867339957011)
XLA Ops:
  0.6 342.9 %shard_map.86 = (bf16[512,2560]{1,0:T(8,128)(2,1)}, f32[2048,128]{1,0:T(8,128)}) custom-call(bf16[2048,2560]{1,0:T(8,128)(2,1)} %tok.1, bf16[2560,128]{1,0:T(8,128)(2,1)} %wq.1, bf16[2560,128]{1,0:T(8,128)(2,1)} %wk.1, bf16[2560,256]{1,0:T(8,128)(2,1)} %wv.1, bf16[2560,128]{1,0:T(8,128)(2,1)} %wg.1, f32[1,128]{1,0:T(1,128)} %bitcast.1, ...), custom_call_target="tpu_custom_call" | custom-call | tf_op jit(solution)/shard_map/pallas_call | solution.py:404
  343.5 0.0 copy-start
  343.5 3.5 %copy.11 = bf16[512,2560]{1,0:T(8,128)(2,1)} copy(bf16[512,2560]{1,0:T(8,128)(2,1)} %get-tuple-element.4) | data formatting | bytes 5242880
  347.0 0.0 copy-done
  347.0 1.0 copy.12
Async XLA Ops:
  343.5 3.5 %copy-start = (f32[2048,128]{1,0:T(8,128)S(1)}, f32[2048,128]{1,0:T(8,128)}, u32[]{:S(2)}) copy-start(f32[2048,128]{1,0:T(8,128)} %get-tuple-element.5) | copy-start | bytes 3145732
where the time goes:
time: 353 us; the launch traced here: 348 us
  Pallas kernels  343 us (97%)
  local copies, waits for them, and re-layouts  4.46 us (1%)
    pallas_call x1, Pallas kernels, body(): pl.pallas_call(functools.partial(kernel, seq, tp, dk, dv, tile, scale), o...  343 us

commit v1 on v0

v1 whole, which is shorter than its diff:
```python
import functools
import math

import jax
import jax.numpy as jnp
from jax import lax
from jax.experimental import pallas as pl
from jax.experimental.pallas import tpu as pltpu
from jax.sharding import PartitionSpec as P

CH = 128
PAD = 8
VMEM_LIMIT = 66 * 1000 * 1000
F32, BF16 = jnp.float32, jnp.bfloat16


def mm(left, right, dims):
    return lax.dot_general(left, right, (dims, ((), ())), preferred_element_type=F32)


NN = ((1,), (0,))
NT = ((1,), (1,))
TN = ((0,), (0,))


def tri_sum(triangle, rows):
    high = rows.astype(BF16)
    low = (rows - high.astype(F32)).astype(BF16)
    return mm(triangle, high, NN) + mm(triangle, low, NN)


def kernel(
    seq, tp, dk, dv, tile, scale,
    tok, wq, wk, wv, wg, rate_ref, dout_ref,
    grad_ref, sig_ref,
    wall, xbuf, proj, sq_all, w_all, s_all, m_all, cl_all, state, msg, got, rep, back, edge,
    wown, land, landd, g_send, g_recv, gmat,
    w_sem, x_sem, e1_s, e1_r, e2_s, e2_r, y_s, y_r, p1_s, p1_r, p2_s, p2_r, dd_s, dd_r, gs_sem, gr_sem,
):
    me, rank = lax.axis_index("seq"), lax.axis_index("tp")
    length, width, group = dout_ref.shape[0], wall.shape[0], 3 * dk + dv
    blocks, tiles = length // CH, length // tile
    each = blocks // tp
    depth, part = width // seq, dv // seq
    side = math.isqrt(seq // 2)
    core, chip = lax.rem(me, 2), me // 2
    x_at, z_at = chip // side, lax.rem(chip, side)
    offs = (1, 3, 2)
    target = tuple(lax.rem(rank + tp - off, tp) for off in offs)

    def seq_at(dx, dz, on):
        return (lax.rem(x_at + dx, side) * side + lax.rem(z_at + dz, side)) * 2 + on

    def first(d):
        return seq_at((1 - core) * d, core * d, core)

    def second(d):
        return seq_at(core * d, (1 - core) * d, core)

    ahead, behind = (first(1), second(1)), (first(side - 1), second(side - 1))
    partner = me + 1 - 2 * core

    def remote(src, dst, send, recv, axis, to):
        return pltpu.make_async_remote_copy(
            src_ref=src, dst_ref=dst, send_sem=send, recv_sem=recv, device_id={axis: to},
            device_id_type=pl.DeviceIdType.MESH,
        )

    def w_cross(j):
        return remote(wown, land.at[j, 0, 0], y_s.at[j], y_r.at[j], "tp", target[j])

    def w_line(j, n):
        half = depth // 2
        if n == 0:
            a, b, to = land.at[j, 0, 0], land.at[j, 0, 3], ahead[0]
        elif n == 1:
            a, b, to = land.at[j, 0, 0], land.at[j, 0, 1], behind[0]
        elif n == 2:
            rows = pl.ds(0, half)
            a, b, to = land.at[j, 0, 3, rows], land.at[j, 0, 2, rows], ahead[0]
        else:
            rows = pl.ds(half, half)
            a, b, to = land.at[j, 0, 1, rows], land.at[j, 0, 2, rows], behind[0]
        return remote(a, b, p1_s.at[j, n], p1_r.at[j, n], "seq", to)

    def w_plane(j, n):
        a = n % 4
        if n < 4:
            src, dst, to = land.at[j, 0, a], land.at[j, 3, a], ahead[1]
        elif n < 8:
            src, dst, to = land.at[j, 0, a], land.at[j, 1, a], behind[1]
        elif a < 2:
            src, dst, to = land.at[j, 3, a], land.at[j, 2, a], ahead[1]
        else:
            src, dst, to = land.at[j, 1, a], land.at[j, 2, a], behind[1]
        return remote(src, dst, p2_s.at[j, n], p2_r.at[j, n], "seq", to)

    def w_pair(j, b):
        return remote(land.at[j, b], landd.at[j, b], dd_s.at[j, b], dd_r.at[j, b], "seq", partner)

    def gather(j, stage):
        if stage == 0:
            w_cross(j).wait_recv()
            w_line(j, 0).start()
            w_line(j, 1).start()
            w_plane(j, 0).start()
            w_plane(j, 4).start()
        elif stage == 1:
            for n in (0, 1):
                w_line(j, n).wait_recv()
                w_line(j, n + 2).start()
            for a in (3, 1):
                w_plane(j, a).start()
                w_plane(j, 4 + a).start()
        elif stage == 2:
            for n in (2, 3):
                w_line(j, n).wait_recv()
            w_plane(j, 2).start()
            w_plane(j, 6).start()
            w_pair(j, 0).start()
        elif stage == 3:
            for a in (0, 3, 1, 2):
                w_plane(j, a).wait_recv()
                w_plane(j, 4 + a).wait_recv()
                w_plane(j, 8 + a).start()
            w_pair(j, 3).start()
            w_pair(j, 1).start()
        else:
            for a in range(4):
                w_plane(j, 8 + a).wait_recv()
            w_pair(j, 2).start()

    events = iter(EVENTS)

    def pump(count):
        for _ in range(count):
            gather(*next(events))

    def x_copy(t, slot):
        return pltpu.make_async_copy(
            tok.at[pl.ds(pl.multiple_of(t * tile, tile), tile), :], xbuf.at[slot], x_sem.at[slot]
        )

    loads = []
    for n, (w, start, size) in enumerate(
        ((wq, 0, dk), (wk, dk, dk), (wv, 2 * dk, dv), (wg, 2 * dk + dv, dk))
    ):
        loads.append(pltpu.make_async_copy(w, wall.at[:, pl.ds(start, size)], w_sem.at[n]))
    for load in loads:
        load.start()
    x_copy(0, 0).start()

    barrier = pltpu.get_barrier_semaphore()
    for d in range(1, seq):
        pl.semaphore_signal(
            barrier, inc=1, device_id={"seq": lax.rem(me + d, seq)},
            device_id_type=pl.DeviceIdType.MESH,
        )
    for other in target:
        pl.semaphore_signal(
            barrier, inc=1, device_id={"tp": other}, device_id_type=pl.DeviceIdType.MESH
        )

    rows_at = lax.broadcasted_iota(jnp.int32, (CH, CH), 0)
    cols_at = lax.broadcasted_iota(jnp.int32, (CH, CH), 1)
    lower = (rows_at >= cols_at).astype(F32)
    lower_b = lower.astype(BF16)
    upper_b = (rows_at <= cols_at).astype(BF16)
    rate = rate_ref[...]

    state[...] = jnp.zeros_like(state)
    for load in loads:
        load.wait()
    wown[...] = wall[pl.ds(pl.multiple_of(me * depth, 16), depth), 0:group].astype(F32)
    pl.semaphore_wait(barrier, seq + tp - 2)
    for j in range(3):
        w_cross(j).start()

    def project(t, total):
        slot = lax.rem(t, 2)

        @pl.when(t + 1 < tiles)
        def _():
            x_copy(t + 1, 1 - slot).start()

        for at, count in ((2, 2), (4, 2), (6, 2)):
            @pl.when(t == at)
            def _():
                pump(count)

        x_copy(t, slot).wait()
        out = mm(xbuf[slot], wall[:, 0:group], NN)
        base = pl.multiple_of(t * tile, tile)
        proj[pl.ds(base, tile), :] = out[:, : 2 * dk + dv].astype(BF16)
        squashed = jax.nn.sigmoid(out[:, 2 * dk + dv :])
        sq_all[pl.ds(base, tile), :] = squashed
        for j in range(tile // CH):
            part = slice(j * CH, (j + 1) * CH)
            b = t * (tile // CH) + j
            within = tri_sum(lower_b, -rate * squashed[part])
            w_all[pl.ds(pl.multiple_of(base + j * CH, CH), CH), :] = within
            closing = within[CH - 1 : CH]
            cl_all[b] = jnp.broadcast_to(closing, (PAD, dk))
            query = out[part, :dk].astype(BF16).astype(F32)
            key = out[part, dk : 2 * dk].astype(BF16).astype(F32)
            value = out[part, 2 * dk : 2 * dk + dv].astype(BF16)
            dout = dout_ref[pl.ds(pl.multiple_of(base + j * CH, CH), CH), :]
            query_scaled = (query * jnp.exp(within)).astype(BF16)
            key_closing = (key * jnp.exp(closing - within)).astype(BF16)
            entering = state[0]
            s_all[b] = entering
            state[0] = jnp.exp(closing) * entering + mm(value, key_closing, TN)
            fed = mm(dout, query_scaled, TN)
            m_all[b] = fed
            state[1] += jnp.exp(total) * fed
            total = total + closing
        return total

    total = lax.fori_loop(0, tiles, project, jnp.zeros((1, dk), F32))

    msg[:, 0:part, :] = state[0].reshape(seq, part, dk)
    msg[:, part : 2 * part, :] = state[1].reshape(seq, part, dk)
    msg[:, 2 * part :, :] = jnp.broadcast_to(jnp.exp(total)[None], (seq, PAD, dk))

    def scatter(d):
        to = lax.rem(me + d, seq)
        return remote(msg.at[to], got.at[d], e1_s.at[d], e1_r.at[d], "seq", to)

    def collect(d):
        to = lax.rem(me + d, seq)
        return remote(rep.at[to], back.at[me], e2_s.at[d], e2_r.at[d], "seq", to)

    def start_all(copy):
        def run(d, carry):
            copy(d).start()
            return carry

        lax.fori_loop(1, seq, run, 0)

    def wait_all(copy):
        def run(d, carry):
            copy(d).wait()
            return carry

        lax.fori_loop(1, seq, run, 0)

    start_all(scatter)
    got[0] = msg[me]
    pump(2)
    wait_all(scatter)

    def fold_states(p, run):
        it = lax.rem(me + seq - p, seq)
        rep[p, 0:part, :] = run
        return got[it, pl.ds(2 * part, 1), :] * run + got[it, pl.ds(0, part), :]

    def fold_grads(n, run):
        p = seq - 1 - n
        it = lax.rem(me + seq - p, seq)
        rep[p, part:, :] = run
        return got[it, pl.ds(2 * part, 1), :] * run + got[it, pl.ds(part, part), :]

    lax.fori_loop(0, seq, fold_states, jnp.zeros((part, dk), F32))
    lax.fori_loop(0, seq, fold_grads, jnp.zeros((part, dk), F32))
    start_all(collect)
    back[me] = rep[me]
    pump(2)
    wait_all(collect)
    edge[0] = back[:, 0:part, :].reshape(dv, dk)
    edge[1] = back[:, part:, :].reshape(dv, dk)

    def enter(b, so_far):
        s_all[b] = s_all[b] + jnp.exp(so_far) * edge[0]
        return so_far + cl_all[b, 0:1, :]

    lax.fori_loop(0, blocks, enter, jnp.zeros((1, dk), F32))

    def leave(j, carry):
        b = blocks - 1 - j
        fed = m_all[b]
        leaving = edge[1]
        m_all[b] = leaving
        edge[1] = jnp.exp(cl_all[b, 0:1, :]) * leaving + fed
        return carry

    lax.fori_loop(0, blocks, leave, 0)

    def grads(b):
        rows = pl.ds(pl.multiple_of(b * CH, CH), CH)
        query = proj[rows, 0:dk].astype(F32)
        key = proj[rows, dk : 2 * dk].astype(F32)
        value = proj[rows, 2 * dk : 2 * dk + dv]
        within, squashed, dout = w_all[rows, :], sq_all[rows, :], dout_ref[rows, :]
        closing = within[CH - 1 : CH]
        state, leaving = s_all[b], m_all[b]
        grow, shrink, rest = jnp.exp(within), jnp.exp(-within), jnp.exp(closing - within)
        query_f, key_f, close_f = query * grow, key * shrink, key * rest
        query_s, key_s, close_s = query_f.astype(BF16), key_f.astype(BF16), close_f.astype(BF16)
        scores = (mm(query_s, key_s, NT) * lower).astype(BF16)
        d_scores = (mm(dout, value, NT) * lower).astype(BF16)
        leaving_b = leaving.astype(BF16)
        d_query_s = mm(dout, state.astype(BF16), NN) + mm(d_scores, key_s, NN)
        d_key_s = mm(d_scores, query_s, TN)
        d_close = mm(value, leaving_b, NN)
        d_value = mm(scores, dout, TN) + mm(close_s, leaving_b, NT)
        d_query = d_query_s * grow
        d_key = d_key_s * shrink + d_close * rest
        at_close = d_close * close_f
        d_within = d_query_s * query_f - d_key_s * key_f - at_close
        d_closing = jnp.sum(at_close, axis=0, keepdims=True) + jnp.exp(closing) * jnp.sum(
            leaving * state, axis=0, keepdims=True
        )
        d_gate = tri_sum(upper_b, d_within) + d_closing
        pre = d_gate * -rate * squashed * (1.0 - squashed)
        sig_ref[rows, :] = pre * scale
        return d_query, d_key, d_value, pre

    bounds = ((0, dk), (dk, 2 * dk), (2 * dk, 2 * dk + dv), (2 * dk + dv, group))

    def copy_g(j, i):
        return remote(
            g_send.at[j, i], g_recv.at[j, i], gs_sem.at[j, i], gr_sem.at[j, i], "tp", target[j]
        )

    def away(i, carry):
        for j in (2, 0, 1):
            for (lo, hi), grad in zip(bounds, grads(target[j] * each + i)):
                g_send[j, i, :, lo:hi] = grad
            copy_g(j, i).start()
        for at in range(each):
            @pl.when(i == at)
            def _():
                pump(1)
        return carry

    lax.fori_loop(0, each, away, 0)

    def home(i, carry):
        rows = pl.ds(pl.multiple_of(i * CH, CH), CH)
        for (lo, hi), grad in zip(bounds, grads(rank * each + i)):
            gmat[rows, lo:hi] = grad.astype(BF16)
        return carry

    lax.fori_loop(0, each, home, 0)

    def unpack(j):
        for b in range(4):
            w_pair(j, b).wait_recv()

        def run(n, carry):
            b, a = n // 4, lax.rem(n, 4)
            for buffer, on in ((land, core), (landd, 1 - core)):
                origin = seq_at(a * (1 - on) + b * on, a * on + b * (1 - on), on)
                rows = pl.ds(pl.multiple_of(origin * depth, 16), depth)
                wall[rows, (j + 1) * group : (j + 2) * group] = buffer[j, b, a].astype(BF16)
            return carry

        lax.fori_loop(0, 16, run, 0)

    unpack(0)
    unpack(1)
    pump(1)
    unpack(2)

    step = 512 if width % 512 == 0 else width

    def finish(h, carry):
        for i in range(2):
            rows = pl.ds(pl.multiple_of((2 * h + i) * CH, CH), CH)
            for j in range(3):
                copy_g(j, 2 * h + i).wait_recv()
                gmat[rows, (j + 1) * group : (j + 2) * group] = g_recv[j, 2 * h + i].astype(BF16)
        rows = pl.ds(pl.multiple_of(h * 2 * CH, 2 * CH), 2 * CH)
        packed = gmat[rows, :]
        for at in range(0, width, step):
            cols = slice(at, at + step)
            grad_ref[rows, cols] = mm(packed, wall[cols, :], NT).astype(BF16)
        return carry

    lax.fori_loop(0, each // 2, finish, 0)

    for j in range(3):
        w_cross(j).wait_send()
        for n in range(4):
            w_line(j, n).wait_send()
            w_pair(j, n).wait_send()
        for n in range(12):
            w_plane(j, n).wait_send()
        for i in range(each):
            copy_g(j, i).wait_send()


EVENTS = (
    (0, 0), (1, 0), (2, 0), (0, 1), (1, 1), (0, 2), (2, 1), (1, 2), (0, 3), (2, 2),
    (0, 4), (1, 3), (1, 4), (2, 3), (2, 4),
)


def solution(mesh):
    seq, tp = mesh.shape["seq"], mesh.shape["tp"]

    def body(tokens, w_query, w_key, w_value, w_gate, gate_rate, out_grad):
        length, width = tokens.shape
        dk, dv = w_query.shape[1], w_value.shape[1]
        blocks, each = length // CH, length // CH // tp
        tile = 2 * CH
        group = 3 * dk + dv
        scale = 4.0 * math.sqrt(length * seq * dk / dv)
        depth, part = width // seq, dv // seq
        hbm = pl.BlockSpec(memory_space=pl.ANY)
        vmem = pl.BlockSpec(memory_space=pltpu.VMEM)
        dma = pltpu.SemaphoreType.DMA
        return pl.pallas_call(
            functools.partial(kernel, seq, tp, dk, dv, tile, scale),
            out_shape=(
                jax.ShapeDtypeStruct((length // tp, width), BF16),
                jax.ShapeDtypeStruct((length, dk), F32),
            ),
            in_specs=[hbm] * 5 + [vmem] * 2,
            out_specs=(vmem, vmem),
            scratch_shapes=[
                pltpu.VMEM((width, tp * group), BF16),
                pltpu.VMEM((2, tile, width), BF16),
                pltpu.VMEM((length, 2 * dk + dv), BF16),
                pltpu.VMEM((length, dk), F32),
                pltpu.VMEM((length, dk), F32),
                pltpu.VMEM((blocks, dv, dk), F32),
                pltpu.VMEM((blocks, dv, dk), F32),
                pltpu.VMEM((blocks, PAD, dk), F32),
                pltpu.VMEM((2, dv, dk), F32),
                pltpu.VMEM((seq, 2 * part + PAD, dk), F32),
                pltpu.VMEM((seq, 2 * part + PAD, dk), F32),
                pltpu.VMEM((seq, 2 * part, dk), F32),
                pltpu.VMEM((seq, 2 * part, dk), F32),
                pltpu.VMEM((2, dv, dk), F32),
                pltpu.VMEM((depth, group), F32),
                pltpu.VMEM((3, 4, 4, depth, group), F32),
                pltpu.VMEM((3, 4, 4, depth, group), F32),
                pltpu.VMEM((3, each, CH, group), F32),
                pltpu.VMEM((3, each, CH, group), F32),
                pltpu.VMEM((length // tp, tp * group), BF16),
            ]
            + [dma((4,)), dma((2,))]
            + [dma((seq,))] * 4
            + [dma((3,))] * 2
            + [dma((3, 4))] * 2
            + [dma((3, 12))] * 2
            + [dma((3, 4))] * 2
            + [dma((3, each))] * 2,
            compiler_params=pltpu.CompilerParams(
                collective_id=0, has_side_effects=True, vmem_limit_bytes=VMEM_LIMIT
            ),
        )(tokens, w_query, w_key, w_value, w_gate, gate_rate.reshape(1, dk), out_grad)

    placed = (
        P("seq", None),
        P(None, "tp"),
        P(None, "tp"),
        P(None, "tp"),
        P(None, "tp"),
        P("tp"),
        P("seq", "tp"),
    )
    return jax.shard_map(
        body,
        mesh=mesh,
        in_specs=placed,
        out_specs=(P(("seq", "tp"), None), P("seq", "tp")),
        check_vma=False,
    )
```

time: 353 us -> 133 us (0.38); the launches traced: 348 us -> 133 us
  Pallas kernels: 343 us -> 128 us
    pallas_call x1, Pallas kernels: 343 us -> 128 us  [body(): pl.pallas_call(functools.partial(kernel, seq, tp, dk, dv, tile, scale), o...]
where the time goes in v1:
time: 133 us
  Pallas kernels  128 us (96%)
  local copies, waits for them, and re-layouts  4.46 us (3%)
    pallas_call x1, Pallas kernels, body(): pl.pallas_call(functools.partial(kernel, seq, tp, dk, dv, tile, scale), o...  128 us
    unnamed x4, local copies, waits for them, and re-layouts  4.46 us

profile of v1, /device:TPU:1, one launch (start us, length us, event | category | flops | bytes accessed | tf_op | source)
XLA Modules:
  0.0 133.1 jit_solution(17690443012478081344)
XLA Ops:
  0.6 128.0 %shard_map.86 = (bf16[512,2560]{1,0:T(8,128)(2,1)}, f32[2048,128]{1,0:T(8,128)}) custom-call(bf16[2048,2560]{1,0:T(8,128)(2,1)} %tok.1, bf16[2560,128]{1,0:T(8,128)(2,1)} %wq.1, bf16[2560,128]{1,0:T(8,128)(2,1)} %wk.1, bf16[2560,256]{1,0:T(8,128)(2,1)} %wv.1, bf16[2560,128]{1,0:T(8,128)(2,1)} %wg.1, f32[1,128]{1,0:T(1,128)} %bitcast.1, ...), custom_call_target="tpu_custom_call" | custom-call | tf_op jit(solution)/shard_map/pallas_call | solution.py:413
  128.6 0.0 copy-start
  128.7 3.5 %copy.11 = bf16[512,2560]{1,0:T(8,128)(2,1)} copy(bf16[512,2560]{1,0:T(8,128)(2,1)} %get-tuple-element.4) | data formatting | bytes 5242880
  132.1 0.0 copy-done
  132.1 1.0 copy.12
Async XLA Ops:
  128.6 3.5 %copy-start = (f32[2048,128]{1,0:T(8,128)S(1)}, f32[2048,128]{1,0:T(8,128)}, u32[]{:S(2)}) copy-start(f32[2048,128]{1,0:T(8,128)} %get-tuple-element.5) | copy-start | bytes 3145732

commit v2 on v1

--- a/solution.py
+++ b/solution.py
@@ -10,7 +10,7 @@
 
 CH = 128
 PAD = 8
-VMEM_LIMIT = 66 * 1000 * 1000
+VMEM_LIMIT = 67_043_328
 F32, BF16 = jnp.float32, jnp.bfloat16
 
 
@@ -33,20 +33,23 @@
     seq, tp, dk, dv, tile, scale,
     tok, wq, wk, wv, wg, rate_ref, dout_ref,
     grad_ref, sig_ref,
-    wall, xbuf, proj, sq_all, w_all, s_all, m_all, cl_all, state, msg, got, rep, back, edge,
-    wown, land, landd, g_send, g_recv, gmat,
-    w_sem, x_sem, e1_s, e1_r, e2_s, e2_r, y_s, y_r, p1_s, p1_r, p2_s, p2_r, dd_s, dd_r, gs_sem, gr_sem,
+    wall, xbuf, out_a, out_b, proj, sq_all, w_all, s_all, m_all, cl_all, state, msg, got, rep, back, edge,
+    wown, land, landd, d_send, d_recv, r_send, r_recv, st_recv, g_send, g_recv, gmat, acc,
+    w_sem, x_sem, e1_s, e1_r, e2_s, e2_r, y_s, y_r, p1_s, p1_r, p2_s, p2_r, dd_s, dd_r,
+    do_s, do_r, ra_s, ra_r, st_s, st_r, gs_sem, gr_sem, met,
 ):
     me, rank = lax.axis_index("seq"), lax.axis_index("tp")
     length, width, group = dout_ref.shape[0], wall.shape[0], 3 * dk + dv
-    blocks, tiles = length // CH, length // tile
+    blocks, pairs = length // CH, length // (2 * tile)
     each = blocks // tp
+    chunk = each * CH
     depth, part = width // seq, dv // seq
     side = math.isqrt(seq // 2)
     core, chip = lax.rem(me, 2), me // 2
     x_at, z_at = chip // side, lax.rem(chip, side)
     offs = (1, 3, 2)
     target = tuple(lax.rem(rank + tp - off, tp) for off in offs)
+    slots = (1, 2, 1)
 
     def seq_at(dx, dz, on):
         return (lax.rem(x_at + dx, side) * side + lax.rem(z_at + dz, side)) * 2 + on
@@ -64,6 +67,11 @@
         return pltpu.make_async_remote_copy(
             src_ref=src, dst_ref=dst, send_sem=send, recv_sem=recv, device_id={axis: to},
             device_id_type=pl.DeviceIdType.MESH,
+        )
+
+    def notify(sem, axis, to):
+        pl.semaphore_signal(
+            sem, inc=1, device_id={axis: to}, device_id_type=pl.DeviceIdType.MESH
         )
 
     def w_cross(j):
@@ -136,9 +144,32 @@
         for _ in range(count):
             gather(*next(events))
 
-    def x_copy(t, slot):
+    def pump_at(i, counts):
+        for at, count in enumerate(counts):
+            if count:
+                @pl.when(i == at)
+                def _():
+                    pump(count)
+
+    def x_copy(k, slot):
         return pltpu.make_async_copy(
-            tok.at[pl.ds(pl.multiple_of(t * tile, tile), tile), :], xbuf.at[slot], x_sem.at[slot]
+            tok.at[pl.ds(pl.multiple_of(k * 2 * tile, 2 * tile), 2 * tile), :], xbuf.at[slot],
+            x_sem.at[slot],
+        )
+
+    def copy_d(j):
+        return remote(d_send.at[j], d_recv.at[j], do_s.at[j], do_r.at[j], "tp", target[j])
+
+    def copy_r(j):
+        return remote(r_send, r_recv.at[j], ra_s.at[j], ra_r.at[j], "tp", target[j])
+
+    def copy_st(j, n):
+        source = (s_all.at[target[j] * each], m_all.at[target[j] * each + each - 1])[n]
+        return remote(source, st_recv.at[j, n], st_s.at[j, n], st_r.at[j, n], "tp", target[j])
+
+    def copy_g(i):
+        return remote(
+            g_send.at[i], g_recv.at[i], gs_sem.at[i], gr_sem.at[i], "tp", target[2]
         )
 
     loads = []
@@ -151,76 +182,96 @@
     x_copy(0, 0).start()
 
     barrier = pltpu.get_barrier_semaphore()
-    for d in range(1, seq):
-        pl.semaphore_signal(
-            barrier, inc=1, device_id={"seq": lax.rem(me + d, seq)},
-            device_id_type=pl.DeviceIdType.MESH,
-        )
-    for other in target:
-        pl.semaphore_signal(
-            barrier, inc=1, device_id={"tp": other}, device_id_type=pl.DeviceIdType.MESH
-        )
+    for d in range(1, side):
+        notify(barrier, "seq", first(d))
+        notify(barrier, "seq", second(d))
+    notify(barrier, "seq", partner)
+    for to in target:
+        notify(barrier, "tp", to)
 
     rows_at = lax.broadcasted_iota(jnp.int32, (CH, CH), 0)
     cols_at = lax.broadcasted_iota(jnp.int32, (CH, CH), 1)
     lower = (rows_at >= cols_at).astype(F32)
     lower_b = lower.astype(BF16)
     upper_b = (rows_at <= cols_at).astype(BF16)
-    rate = rate_ref[...]
+    own_rate = rate_ref[...]
 
     state[...] = jnp.zeros_like(state)
+    out_b[...] = jnp.zeros_like(out_b)
+    r_send[...] = jnp.broadcast_to(own_rate, (PAD, dk))
+    for j in range(2):
+        rows = pl.ds(pl.multiple_of(target[j] * chunk, chunk), chunk)
+        d_send[j] = dout_ref[rows, :].astype(F32)
     for load in loads:
         load.wait()
     wown[...] = wall[pl.ds(pl.multiple_of(me * depth, 16), depth), 0:group].astype(F32)
-    pl.semaphore_wait(barrier, seq + tp - 2)
+    pl.semaphore_wait(barrier, 2 * side - 1 + tp - 1)
     for j in range(3):
         w_cross(j).start()
-
-    def project(t, total):
-        slot = lax.rem(t, 2)
-
-        @pl.when(t + 1 < tiles)
-        def _():
-            x_copy(t + 1, 1 - slot).start()
-
-        for at, count in ((2, 2), (4, 2), (6, 2)):
-            @pl.when(t == at)
-            def _():
-                pump(count)
-
-        x_copy(t, slot).wait()
-        out = mm(xbuf[slot], wall[:, 0:group], NN)
+    for j in range(2):
+        copy_r(j).start()
+        copy_d(j).start()
+    for d in range(1, side):
+        notify(met.at[0], "seq", first(d))
+
+    def post(out, t, rate, total, dout_at, slope):
         base = pl.multiple_of(t * tile, tile)
         proj[pl.ds(base, tile), :] = out[:, : 2 * dk + dv].astype(BF16)
         squashed = jax.nn.sigmoid(out[:, 2 * dk + dv :])
         sq_all[pl.ds(base, tile), :] = squashed
-        for j in range(tile // CH):
-            part = slice(j * CH, (j + 1) * CH)
-            b = t * (tile // CH) + j
-            within = tri_sum(lower_b, -rate * squashed[part])
-            w_all[pl.ds(pl.multiple_of(base + j * CH, CH), CH), :] = within
+        for n in range(tile // CH):
+            here = slice(n * CH, (n + 1) * CH)
+            b = t * (tile // CH) + n
+            within = tri_sum(lower_b, -rate * squashed[here])
+            rows = pl.ds(pl.multiple_of(base + n * CH, CH), CH)
+            w_all[rows, :] = within
             closing = within[CH - 1 : CH]
             cl_all[b] = jnp.broadcast_to(closing, (PAD, dk))
-            query = out[part, :dk].astype(BF16).astype(F32)
-            key = out[part, dk : 2 * dk].astype(BF16).astype(F32)
-            value = out[part, 2 * dk : 2 * dk + dv].astype(BF16)
-            dout = dout_ref[pl.ds(pl.multiple_of(base + j * CH, CH), CH), :]
+            query = out[here, :dk].astype(BF16).astype(F32)
+            key = out[here, dk : 2 * dk].astype(BF16).astype(F32)
+            value = out[here, 2 * dk : 2 * dk + dv].astype(BF16)
             query_scaled = (query * jnp.exp(within)).astype(BF16)
             key_closing = (key * jnp.exp(closing - within)).astype(BF16)
             entering = state[0]
             s_all[b] = entering
             state[0] = jnp.exp(closing) * entering + mm(value, key_closing, TN)
-            fed = mm(dout, query_scaled, TN)
+            fed = mm(dout_at(rows), query_scaled, TN)
             m_all[b] = fed
-            state[1] += jnp.exp(total) * fed
-            total = total + closing
+            if slope is not None:
+                state[1] += jnp.exp(total) * fed
+                total = total + slope * closing
         return total
 
-    total = lax.fori_loop(0, tiles, project, jnp.zeros((1, dk), F32))
+    def own_dout(rows):
+        return dout_ref[rows, :]
+
+    def project(k, total):
+        slot = lax.rem(k, 2)
+        x_copy(k, slot).wait()
+
+        @pl.when(k + 1 < pairs)
+        def _():
+            x_copy(k + 1, 1 - slot).start()
+
+        pump_at(k, PUMPS_PROJECT)
+        out_a[...] = mm(xbuf[slot, 0:tile], wall[:, 0:group], NN)
+        total = post(
+            out_b, jnp.maximum(2 * k - 1, 0), own_rate, total, own_dout,
+            jnp.minimum(k, 1).astype(F32),
+        )
+        out_b[...] = mm(xbuf[slot, tile : 2 * tile], wall[:, 0:group], NN)
+        return post(out_a, 2 * k, own_rate, total, own_dout, 1.0)
+
+    total = lax.fori_loop(0, pairs, project, jnp.zeros((1, dk), F32))
+    pl.semaphore_wait(met.at[0], side - 1)
+    notify(met.at[1], "seq", partner)
+    total = post(out_b, 2 * pairs - 1, own_rate, total, own_dout, 1.0)
+    x_copy(rank, 0).start()
 
     msg[:, 0:part, :] = state[0].reshape(seq, part, dk)
     msg[:, part : 2 * part, :] = state[1].reshape(seq, part, dk)
     msg[:, 2 * part :, :] = jnp.broadcast_to(jnp.exp(total)[None], (seq, PAD, dk))
+    pl.semaphore_wait(met.at[1], 1)
 
     def scatter(d):
         to = lax.rem(me + d, seq)
@@ -246,7 +297,7 @@
 
     start_all(scatter)
     got[0] = msg[me]
-    pump(2)
+    pump(PUMP_SCATTER)
     wait_all(scatter)
 
     def fold_states(p, run):
@@ -264,7 +315,7 @@
     lax.fori_loop(0, seq, fold_grads, jnp.zeros((part, dk), F32))
     start_all(collect)
     back[me] = rep[me]
-    pump(2)
+    pump(PUMP_COLLECT)
     wait_all(collect)
     edge[0] = back[:, 0:part, :].reshape(dv, dk)
     edge[1] = back[:, part:, :].reshape(dv, dk)
@@ -275,75 +326,93 @@
 
     lax.fori_loop(0, blocks, enter, jnp.zeros((1, dk), F32))
 
-    def leave(j, carry):
-        b = blocks - 1 - j
-        fed = m_all[b]
-        leaving = edge[1]
-        m_all[b] = leaving
-        edge[1] = jnp.exp(cl_all[b, 0:1, :]) * leaving + fed
-        return carry
-
-    lax.fori_loop(0, blocks, leave, 0)
-
-    def grads(b):
+    def leave_from(count):
+        def leave(n, carry):
+            b = count - 1 - n
+            fed = m_all[b]
+            leaving = edge[1]
+            m_all[b] = leaving
+            edge[1] = jnp.exp(cl_all[b, 0:1, :]) * leaving + fed
+            return carry
+
+        lax.fori_loop(0, count, leave, 0)
+
+    leave_from(blocks)
+    for j in range(2):
+        copy_st(j, 0).start()
+        copy_st(j, 1).start()
+
+    def grads(b, rate, dout_at, whole):
         rows = pl.ds(pl.multiple_of(b * CH, CH), CH)
         query = proj[rows, 0:dk].astype(F32)
         key = proj[rows, dk : 2 * dk].astype(F32)
         value = proj[rows, 2 * dk : 2 * dk + dv]
-        within, squashed, dout = w_all[rows, :], sq_all[rows, :], dout_ref[rows, :]
+        within, squashed, dout = w_all[rows, :], sq_all[rows, :], dout_at(rows)
         closing = within[CH - 1 : CH]
-        state, leaving = s_all[b], m_all[b]
+        entering, leaving = s_all[b], m_all[b]
         grow, shrink, rest = jnp.exp(within), jnp.exp(-within), jnp.exp(closing - within)
         query_f, key_f, close_f = query * grow, key * shrink, key * rest
         query_s, key_s, close_s = query_f.astype(BF16), key_f.astype(BF16), close_f.astype(BF16)
-        scores = (mm(query_s, key_s, NT) * lower).astype(BF16)
         d_scores = (mm(dout, value, NT) * lower).astype(BF16)
         leaving_b = leaving.astype(BF16)
-        d_query_s = mm(dout, state.astype(BF16), NN) + mm(d_scores, key_s, NN)
+        d_query_s = mm(dout, entering.astype(BF16), NN) + mm(d_scores, key_s, NN)
         d_key_s = mm(d_scores, query_s, TN)
         d_close = mm(value, leaving_b, NN)
-        d_value = mm(scores, dout, TN) + mm(close_s, leaving_b, NT)
-        d_query = d_query_s * grow
-        d_key = d_key_s * shrink + d_close * rest
         at_close = d_close * close_f
         d_within = d_query_s * query_f - d_key_s * key_f - at_close
         d_closing = jnp.sum(at_close, axis=0, keepdims=True) + jnp.exp(closing) * jnp.sum(
-            leaving * state, axis=0, keepdims=True
+            leaving * entering, axis=0, keepdims=True
         )
         d_gate = tri_sum(upper_b, d_within) + d_closing
         pre = d_gate * -rate * squashed * (1.0 - squashed)
-        sig_ref[rows, :] = pre * scale
+        if not whole:
+            return pre
+        scores = (mm(query_s, key_s, NT) * lower).astype(BF16)
+        d_query = d_query_s * grow
+        d_key = d_key_s * shrink + d_close * rest
+        d_value = mm(scores, dout, TN) + mm(close_s, leaving_b, NT)
         return d_query, d_key, d_value, pre
 
     bounds = ((0, dk), (dk, 2 * dk), (2 * dk, 2 * dk + dv), (2 * dk + dv, group))
 
-    def copy_g(j, i):
-        return remote(
-            g_send.at[j, i], g_recv.at[j, i], gs_sem.at[j, i], gr_sem.at[j, i], "tp", target[j]
-        )
+    def signal_of(b, pre):
+        sig_ref[pl.ds(pl.multiple_of(b * CH, CH), CH), :] = pre * scale
 
     def away(i, carry):
-        for j in (2, 0, 1):
-            for (lo, hi), grad in zip(bounds, grads(target[j] * each + i)):
-                g_send[j, i, :, lo:hi] = grad
-            copy_g(j, i).start()
-        for at in range(each):
-            @pl.when(i == at)
-            def _():
-                pump(1)
+        b = target[2] * each + i
+        found = grads(b, own_rate, own_dout, True)
+        signal_of(b, found[3])
+        for (lo, hi), grad in zip(bounds, found):
+            g_send[i, :, lo:hi] = grad
+        copy_g(i).start()
+        pump_at(i, PUMPS_AWAY)
         return carry
 
     lax.fori_loop(0, each, away, 0)
 
     def home(i, carry):
+        b = rank * each + i
+        found = grads(b, own_rate, own_dout, True)
+        signal_of(b, found[3])
         rows = pl.ds(pl.multiple_of(i * CH, CH), CH)
-        for (lo, hi), grad in zip(bounds, grads(rank * each + i)):
+        for (lo, hi), grad in zip(bounds, found):
             gmat[rows, lo:hi] = grad.astype(BF16)
+        pump_at(i, PUMPS_HOME)
         return carry
 
     lax.fori_loop(0, each, home, 0)
 
+    def aside(i, carry):
+        for j in range(2):
+            b = target[j] * each + i
+            signal_of(b, grads(b, own_rate, own_dout, False))
+        pump_at(i, PUMPS_ASIDE)
+        return carry
+
+    lax.fori_loop(0, each, aside, 0)
+
     def unpack(j):
+        start = slots[j] * group
         for b in range(4):
             w_pair(j, b).wait_recv()
 
@@ -352,32 +421,68 @@
             for buffer, on in ((land, core), (landd, 1 - core)):
                 origin = seq_at(a * (1 - on) + b * on, a * on + b * (1 - on), on)
                 rows = pl.ds(pl.multiple_of(origin * depth, 16), depth)
-                wall[rows, (j + 1) * group : (j + 2) * group] = buffer[j, b, a].astype(BF16)
+                wall[rows, start : start + group] = buffer[j, b, a].astype(BF16)
             return carry
 
         lax.fori_loop(0, 16, run, 0)
 
-    unpack(0)
-    unpack(1)
-    pump(1)
+    x_copy(rank, 0).wait()
+    for j in range(2):
+        for n in range(2):
+            copy_st(j, n).wait_send()
+
+    def near(j):
+        start = slots[j] * group
+        unpack(j)
+        copy_r(j).wait_recv()
+        copy_d(j).wait_recv()
+        for n in range(2):
+            copy_st(j, n).wait_recv()
+        rate = r_recv[j, 0:1, :]
+
+        def dout_at(rows):
+            return d_recv[j, rows, :].astype(BF16)
+
+        state[0] = st_recv[j, 0]
+        edge[1] = st_recv[j, 1]
+        out_a[...] = mm(xbuf[0, 0:tile], wall[:, start : start + group], NN)
+        out_b[...] = mm(xbuf[0, tile : 2 * tile], wall[:, start : start + group], NN)
+        post(out_a, 0, rate, None, dout_at, None)
+        post(out_b, 1, rate, None, dout_at, None)
+        leave_from(each)
+
+        def run(i, carry):
+            rows = pl.ds(pl.multiple_of(i * CH, CH), CH)
+            for (lo, hi), grad in zip(bounds, grads(i, rate, dout_at, True)):
+                gmat[rows, (j + 1) * group + lo : (j + 1) * group + hi] = grad.astype(BF16)
+            return carry
+
+        lax.fori_loop(0, each, run, 0)
+
+    near(0)
+    pump(PUMP_NEAR)
+    near(1)
+
+    step = 512 if width % 512 == 0 else width
+
+    def gather_own(n, carry):
+        cols = pl.ds(pl.multiple_of(n * step, step), step)
+        acc[n] = mm(gmat[...], wall[cols, :], NT)
+        return carry
+
+    lax.fori_loop(0, width // step, gather_own, 0)
+    for event in events:
+        gather(*event)
     unpack(2)
-
-    step = 512 if width % 512 == 0 else width
-
-    def finish(h, carry):
-        for i in range(2):
-            rows = pl.ds(pl.multiple_of((2 * h + i) * CH, CH), CH)
-            for j in range(3):
-                copy_g(j, 2 * h + i).wait_recv()
-                gmat[rows, (j + 1) * group : (j + 2) * group] = g_recv[j, 2 * h + i].astype(BF16)
-        rows = pl.ds(pl.multiple_of(h * 2 * CH, 2 * CH), 2 * CH)
-        packed = gmat[rows, :]
-        for at in range(0, width, step):
-            cols = slice(at, at + step)
-            grad_ref[rows, cols] = mm(packed, wall[cols, :], NT).astype(BF16)
-        return carry
-
-    lax.fori_loop(0, each // 2, finish, 0)
+    for i in range(each):
+        copy_g(i).wait_recv()
+        gmat[i * CH : (i + 1) * CH, 0:group] = g_recv[i].astype(BF16)
+    start = slots[2] * group
+    for n in range(width // step):
+        cols = slice(n * step, (n + 1) * step)
+        grad_ref[:, cols] = (
+            acc[n] + mm(gmat[:, 0:group], wall[cols, start : start + group], NT)
+        ).astype(BF16)
 
     for j in range(3):
         w_cross(j).wait_send()
@@ -386,14 +491,24 @@
             w_pair(j, n).wait_send()
         for n in range(12):
             w_plane(j, n).wait_send()
-        for i in range(each):
-            copy_g(j, i).wait_send()
+    for j in range(2):
+        copy_r(j).wait_send()
+        copy_d(j).wait_send()
+    for i in range(each):
+        copy_g(i).wait_send()
 
 
 EVENTS = (
-    (0, 0), (1, 0), (2, 0), (0, 1), (1, 1), (0, 2), (2, 1), (1, 2), (0, 3), (2, 2),
-    (0, 4), (1, 3), (1, 4), (2, 3), (2, 4),
+    (0, 0), (1, 0), (2, 0), (0, 1), (1, 1), (2, 1), (0, 2), (1, 2), (2, 2),
+    (0, 3), (0, 4), (1, 3), (1, 4), (2, 3), (2, 4),
 )
+PUMPS_PROJECT = (0, 0, 2, 0)
+PUMP_SCATTER = 3
+PUMP_COLLECT = 3
+PUMPS_AWAY = (0, 0, 1, 1)
+PUMPS_HOME = (0, 0, 0, 1)
+PUMPS_ASIDE = (0, 0, 0, 1)
+PUMP_NEAR = 2
 
 
 def solution(mesh):
@@ -405,22 +520,26 @@
         blocks, each = length // CH, length // CH // tp
         tile = 2 * CH
         group = 3 * dk + dv
+        chunk = each * CH
         scale = 4.0 * math.sqrt(length * seq * dk / dv)
         depth, part = width // seq, dv // seq
+        step = 512 if width % 512 == 0 else width
         hbm = pl.BlockSpec(memory_space=pl.ANY)
         vmem = pl.BlockSpec(memory_space=pltpu.VMEM)
         dma = pltpu.SemaphoreType.DMA
         return pl.pallas_call(
             functools.partial(kernel, seq, tp, dk, dv, tile, scale),
             out_shape=(
-                jax.ShapeDtypeStruct((length // tp, width), BF16),
+                jax.ShapeDtypeStruct((chunk, width), BF16),
                 jax.ShapeDtypeStruct((length, dk), F32),
             ),
             in_specs=[hbm] * 5 + [vmem] * 2,
             out_specs=(vmem, vmem),
             scratch_shapes=[
-                pltpu.VMEM((width, tp * group), BF16),
-                pltpu.VMEM((2, tile, width), BF16),
+                pltpu.VMEM((width, 3 * group), BF16),
+                pltpu.VMEM((2, 2 * tile, width), BF16),
+                pltpu.VMEM((tile, group), F32),
+                pltpu.VMEM((tile, group), F32),
                 pltpu.VMEM((length, 2 * dk + dv), BF16),
                 pltpu.VMEM((length, dk), F32),
                 pltpu.VMEM((length, dk), F32),
@@ -436,9 +555,15 @@
                 pltpu.VMEM((depth, group), F32),
                 pltpu.VMEM((3, 4, 4, depth, group), F32),
                 pltpu.VMEM((3, 4, 4, depth, group), F32),
-                pltpu.VMEM((3, each, CH, group), F32),
-                pltpu.VMEM((3, each, CH, group), F32),
-                pltpu.VMEM((length // tp, tp * group), BF16),
+                pltpu.VMEM((2, chunk, dv), F32),
+                pltpu.VMEM((2, chunk, dv), F32),
+                pltpu.VMEM((PAD, dk), F32),
+                pltpu.VMEM((2, PAD, dk), F32),
+                pltpu.VMEM((2, 2, dv, dk), F32),
+                pltpu.VMEM((each, CH, group), F32),
+                pltpu.VMEM((each, CH, group), F32),
+                pltpu.VMEM((chunk, 3 * group), BF16),
+                pltpu.VMEM((width // step, chunk, step), F32),
             ]
             + [dma((4,)), dma((2,))]
             + [dma((seq,))] * 4
@@ -446,7 +571,10 @@
             + [dma((3, 4))] * 2
             + [dma((3, 12))] * 2
             + [dma((3, 4))] * 2
-            + [dma((3, each))] * 2,
+            + [dma((2,))] * 4
+            + [dma((2, 2))] * 2
+            + [dma((each,))] * 2
+            + [pltpu.SemaphoreType.REGULAR((2,))],
             compiler_params=pltpu.CompilerParams(
                 collective_id=0, has_side_effects=True, vmem_limit_bytes=VMEM_LIMIT
             ),

time: 133 us -> 125 us (0.940)
  Pallas kernels: 128 us -> 120 us
    pallas_call x1, Pallas kernels: 128 us -> 120 us  [body(): pl.pallas_call(functools.partial(kernel, seq, tp, dk, dv, tile, scale), o...]
where the time goes in v2:
time: 125 us
  Pallas kernels  120 us (96%)
  local copies, waits for them, and re-layouts  4.46 us (4%)
    pallas_call x1, Pallas kernels, body(): pl.pallas_call(functools.partial(kernel, seq, tp, dk, dv, tile, scale), o...  120 us
    unnamed x4, local copies, waits for them, and re-layouts  4.46 us

profile of v2, /device:TPU:1, one launch (start us, length us, event | category | flops | bytes accessed | tf_op | source)
XLA Modules:
  0.0 124.9 jit_solution(2938249453289501424)
XLA Ops:
  0.6 119.8 %shard_map.86 = (bf16[512,2560]{1,0:T(8,128)(2,1)}, f32[2048,128]{1,0:T(8,128)}) custom-call(bf16[2048,2560]{1,0:T(8,128)(2,1)} %tok.1, bf16[2560,128]{1,0:T(8,128)(2,1)} %wq.1, bf16[2560,128]{1,0:T(8,128)(2,1)} %wk.1, bf16[2560,256]{1,0:T(8,128)(2,1)} %wv.1, bf16[2560,128]{1,0:T(8,128)(2,1)} %wg.1, f32[1,128]{1,0:T(1,128)} %bitcast.1, ...), custom_call_target="tpu_custom_call" | custom-call | tf_op jit(solution)/shard_map/pallas_call | solution.py:530
  120.5 0.0 copy-start
  120.5 3.5 %copy.11 = bf16[512,2560]{1,0:T(8,128)(2,1)} copy(bf16[512,2560]{1,0:T(8,128)(2,1)} %get-tuple-element.4) | data formatting | bytes 5242880
  124.0 0.0 copy-done
  124.0 1.0 copy.12
Async XLA Ops:
  120.5 3.5 %copy-start = (f32[2048,128]{1,0:T(8,128)S(1)}, f32[2048,128]{1,0:T(8,128)}, u32[]{:S(2)}) copy-start(f32[2048,128]{1,0:T(8,128)} %get-tuple-element.5) | copy-start | bytes 3145732

commit v3 on v2

--- a/solution.py
+++ b/solution.py
@@ -31,18 +31,20 @@
 
 def kernel(
     seq, tp, dk, dv, tile, scale,
-    tok, wq, wk, wv, wg, rate_ref, dout_ref,
-    grad_ref, sig_ref,
-    wall, xbuf, out_a, out_b, proj, sq_all, w_all, s_all, m_all, cl_all, state, msg, got, rep, back, edge,
-    wown, land, landd, d_send, d_recv, r_send, r_recv, st_recv, g_send, g_recv, gmat, acc,
-    w_sem, x_sem, e1_s, e1_r, e2_s, e2_r, y_s, y_r, p1_s, p1_r, p2_s, p2_r, dd_s, dd_r,
-    do_s, do_r, ra_s, ra_r, st_s, st_r, gs_sem, gr_sem, met,
+    tok, wq, wk, wv, wg, rate_ref, dout_in,
+    grad_out, sig_out,
+    wall, xbuf, out_a, out_b, dout_ref, sig_ref, grad_ref, proj, sq_all, w_all, s_all, m_all, cl_all,
+    proj_n, sq_n, w_n, s_n, m_n, cl_n, state, msg, got, rep, back, edge,
+    wown, land, landd, d_send, d_recv, r_send, r_recv, st_recv, gmat, acc,
+    w_sem, x_sem, o_sem, e1_s, e1_r, e2_s, e2_r, y_s, y_r, p1_s, p1_r, p2_s, p2_r, dd_s, dd_r,
+    do_s, do_r, ra_s, ra_r, st_s, st_r, met,
 ):
     me, rank = lax.axis_index("seq"), lax.axis_index("tp")
     length, width, group = dout_ref.shape[0], wall.shape[0], 3 * dk + dv
     blocks, pairs = length // CH, length // (2 * tile)
     each = blocks // tp
     chunk = each * CH
+    step = 512 if width % 512 == 0 else width
     depth, part = width // seq, dv // seq
     side = math.isqrt(seq // 2)
     core, chip = lax.rem(me, 2), me // 2
@@ -50,6 +52,8 @@
     offs = (1, 3, 2)
     target = tuple(lax.rem(rank + tp - off, tp) for off in offs)
     slots = (1, 2, 1)
+    own = (proj, sq_all, w_all, s_all, m_all, cl_all)
+    other = (proj_n, sq_n, w_n, s_n, m_n, cl_n)
 
     def seq_at(dx, dz, on):
         return (lax.rem(x_at + dx, side) * side + lax.rem(z_at + dz, side)) * 2 + on
@@ -127,29 +131,25 @@
             w_plane(j, 6).start()
             w_pair(j, 0).start()
         elif stage == 3:
-            for a in (0, 3, 1, 2):
+            for a in (0, 3):
+                w_plane(j, a).wait_recv()
+                w_plane(j, 4 + a).wait_recv()
+                w_plane(j, 8 + a).start()
+        elif stage == 4:
+            for a in (1, 2):
                 w_plane(j, a).wait_recv()
                 w_plane(j, 4 + a).wait_recv()
                 w_plane(j, 8 + a).start()
             w_pair(j, 3).start()
             w_pair(j, 1).start()
-        else:
+        elif stage == 5:
             for a in range(4):
                 w_plane(j, 8 + a).wait_recv()
             w_pair(j, 2).start()
-
-    events = iter(EVENTS)
-
-    def pump(count):
-        for _ in range(count):
-            gather(*next(events))
-
-    def pump_at(i, counts):
-        for at, count in enumerate(counts):
-            if count:
-                @pl.when(i == at)
-                def _():
-                    pump(count)
+        elif stage == 6:
+            w_cross(j).start()
+        else:
+            copy_d(j).start()
 
     def x_copy(k, slot):
         return pltpu.make_async_copy(
@@ -167,10 +167,13 @@
         source = (s_all.at[target[j] * each], m_all.at[target[j] * each + each - 1])[n]
         return remote(source, st_recv.at[j, n], st_s.at[j, n], st_r.at[j, n], "tp", target[j])
 
-    def copy_g(i):
-        return remote(
-            g_send.at[i], g_recv.at[i], gs_sem.at[i], gr_sem.at[i], "tp", target[2]
-        )
+    def copy_sig(i):
+        rows = pl.ds(pl.multiple_of(i * chunk, chunk), chunk)
+        return pltpu.make_async_copy(sig_ref.at[rows], sig_out.at[rows], o_sem.at[i])
+
+    def copy_grad(n):
+        cols = pl.ds(n * step, step)
+        return pltpu.make_async_copy(grad_ref.at[:, cols], grad_out.at[:, cols], o_sem.at[tp + n])
 
     loads = []
     for n, (w, start, size) in enumerate(
@@ -179,6 +182,8 @@
         loads.append(pltpu.make_async_copy(w, wall.at[:, pl.ds(start, size)], w_sem.at[n]))
     for load in loads:
         load.start()
+    dout_load = pltpu.make_async_copy(dout_in, dout_ref, w_sem.at[4])
+    dout_load.start()
     x_copy(0, 0).start()
 
     barrier = pltpu.get_barrier_semaphore()
@@ -199,22 +204,23 @@
     state[...] = jnp.zeros_like(state)
     out_b[...] = jnp.zeros_like(out_b)
     r_send[...] = jnp.broadcast_to(own_rate, (PAD, dk))
-    for j in range(2):
-        rows = pl.ds(pl.multiple_of(target[j] * chunk, chunk), chunk)
-        d_send[j] = dout_ref[rows, :].astype(F32)
     for load in loads:
         load.wait()
     wown[...] = wall[pl.ds(pl.multiple_of(me * depth, 16), depth), 0:group].astype(F32)
     pl.semaphore_wait(barrier, 2 * side - 1 + tp - 1)
+    for j in range(2):
+        w_cross(j).start()
     for j in range(3):
-        w_cross(j).start()
-    for j in range(2):
         copy_r(j).start()
-        copy_d(j).start()
     for d in range(1, side):
         notify(met.at[0], "seq", first(d))
-
-    def post(out, t, rate, total, dout_at, slope):
+    dout_load.wait()
+    for j in range(3):
+        rows = pl.ds(pl.multiple_of(target[j] * chunk, chunk), chunk)
+        d_send[j] = dout_ref[rows, :].astype(F32)
+
+    def post(out, t, kept, rate, total, dout_at, slope):
+        proj, sq_all, w_all, s_all, m_all, cl_all = kept
         base = pl.multiple_of(t * tile, tile)
         proj[pl.ds(base, tile), :] = out[:, : 2 * dk + dv].astype(BF16)
         squashed = jax.nn.sigmoid(out[:, 2 * dk + dv :])
@@ -253,19 +259,23 @@
         def _():
             x_copy(k + 1, 1 - slot).start()
 
-        pump_at(k, PUMPS_PROJECT)
+        for at, *event in EARLY:
+            @pl.when(k == at)
+            def _():
+                gather(*event)
+
         out_a[...] = mm(xbuf[slot, 0:tile], wall[:, 0:group], NN)
         total = post(
-            out_b, jnp.maximum(2 * k - 1, 0), own_rate, total, own_dout,
+            out_b, jnp.maximum(2 * k - 1, 0), own, own_rate, total, own_dout,
             jnp.minimum(k, 1).astype(F32),
         )
         out_b[...] = mm(xbuf[slot, tile : 2 * tile], wall[:, 0:group], NN)
-        return post(out_a, 2 * k, own_rate, total, own_dout, 1.0)
+        return post(out_a, 2 * k, own, own_rate, total, own_dout, 1.0)
 
     total = lax.fori_loop(0, pairs, project, jnp.zeros((1, dk), F32))
     pl.semaphore_wait(met.at[0], side - 1)
     notify(met.at[1], "seq", partner)
-    total = post(out_b, 2 * pairs - 1, own_rate, total, own_dout, 1.0)
+    total = post(out_b, 2 * pairs - 1, own, own_rate, total, own_dout, 1.0)
     x_copy(rank, 0).start()
 
     msg[:, 0:part, :] = state[0].reshape(seq, part, dk)
@@ -273,60 +283,13 @@
     msg[:, 2 * part :, :] = jnp.broadcast_to(jnp.exp(total)[None], (seq, PAD, dk))
     pl.semaphore_wait(met.at[1], 1)
 
-    def scatter(d):
-        to = lax.rem(me + d, seq)
-        return remote(msg.at[to], got.at[d], e1_s.at[d], e1_r.at[d], "seq", to)
-
-    def collect(d):
-        to = lax.rem(me + d, seq)
-        return remote(rep.at[to], back.at[me], e2_s.at[d], e2_r.at[d], "seq", to)
-
-    def start_all(copy):
-        def run(d, carry):
-            copy(d).start()
-            return carry
-
-        lax.fori_loop(1, seq, run, 0)
-
-    def wait_all(copy):
-        def run(d, carry):
-            copy(d).wait()
-            return carry
-
-        lax.fori_loop(1, seq, run, 0)
-
-    start_all(scatter)
-    got[0] = msg[me]
-    pump(PUMP_SCATTER)
-    wait_all(scatter)
-
-    def fold_states(p, run):
-        it = lax.rem(me + seq - p, seq)
-        rep[p, 0:part, :] = run
-        return got[it, pl.ds(2 * part, 1), :] * run + got[it, pl.ds(0, part), :]
-
-    def fold_grads(n, run):
-        p = seq - 1 - n
-        it = lax.rem(me + seq - p, seq)
-        rep[p, part:, :] = run
-        return got[it, pl.ds(2 * part, 1), :] * run + got[it, pl.ds(part, part), :]
-
-    lax.fori_loop(0, seq, fold_states, jnp.zeros((part, dk), F32))
-    lax.fori_loop(0, seq, fold_grads, jnp.zeros((part, dk), F32))
-    start_all(collect)
-    back[me] = rep[me]
-    pump(PUMP_COLLECT)
-    wait_all(collect)
-    edge[0] = back[:, 0:part, :].reshape(dv, dk)
-    edge[1] = back[:, part:, :].reshape(dv, dk)
-
-    def enter(b, so_far):
-        s_all[b] = s_all[b] + jnp.exp(so_far) * edge[0]
-        return so_far + cl_all[b, 0:1, :]
-
-    lax.fori_loop(0, blocks, enter, jnp.zeros((1, dk), F32))
-
-    def leave_from(count):
+    def enter_leave(kept, count):
+        s_all, m_all, cl_all = kept[3:]
+
+        def enter(b, so_far):
+            s_all[b] = s_all[b] + jnp.exp(so_far) * edge[0]
+            return so_far + cl_all[b, 0:1, :]
+
         def leave(n, carry):
             b = count - 1 - n
             fed = m_all[b]
@@ -335,14 +298,11 @@
             edge[1] = jnp.exp(cl_all[b, 0:1, :]) * leaving + fed
             return carry
 
+        lax.fori_loop(0, count, enter, jnp.zeros((1, dk), F32))
         lax.fori_loop(0, count, leave, 0)
 
-    leave_from(blocks)
-    for j in range(2):
-        copy_st(j, 0).start()
-        copy_st(j, 1).start()
-
-    def grads(b, rate, dout_at, whole):
+    def grads(b, kept, rate, dout_at, whole):
+        proj, sq_all, w_all, s_all, m_all, cl_all = kept
         rows = pl.ds(pl.multiple_of(b * CH, CH), CH)
         query = proj[rows, 0:dk].astype(F32)
         key = proj[rows, dk : 2 * dk].astype(F32)
@@ -375,42 +335,6 @@
 
     bounds = ((0, dk), (dk, 2 * dk), (2 * dk, 2 * dk + dv), (2 * dk + dv, group))
 
-    def signal_of(b, pre):
-        sig_ref[pl.ds(pl.multiple_of(b * CH, CH), CH), :] = pre * scale
-
-    def away(i, carry):
-        b = target[2] * each + i
-        found = grads(b, own_rate, own_dout, True)
-        signal_of(b, found[3])
-        for (lo, hi), grad in zip(bounds, found):
-            g_send[i, :, lo:hi] = grad
-        copy_g(i).start()
-        pump_at(i, PUMPS_AWAY)
-        return carry
-
-    lax.fori_loop(0, each, away, 0)
-
-    def home(i, carry):
-        b = rank * each + i
-        found = grads(b, own_rate, own_dout, True)
-        signal_of(b, found[3])
-        rows = pl.ds(pl.multiple_of(i * CH, CH), CH)
-        for (lo, hi), grad in zip(bounds, found):
-            gmat[rows, lo:hi] = grad.astype(BF16)
-        pump_at(i, PUMPS_HOME)
-        return carry
-
-    lax.fori_loop(0, each, home, 0)
-
-    def aside(i, carry):
-        for j in range(2):
-            b = target[j] * each + i
-            signal_of(b, grads(b, own_rate, own_dout, False))
-        pump_at(i, PUMPS_ASIDE)
-        return carry
-
-    lax.fori_loop(0, each, aside, 0)
-
     def unpack(j):
         start = slots[j] * group
         for b in range(4):
@@ -426,89 +350,174 @@
 
         lax.fori_loop(0, 16, run, 0)
 
-    x_copy(rank, 0).wait()
-    for j in range(2):
-        for n in range(2):
-            copy_st(j, n).wait_send()
-
     def near(j):
         start = slots[j] * group
-        unpack(j)
+        def dout_at(rows):
+            return d_recv[j, rows, :].astype(BF16)
+
+        def before():
+            unpack(j)
+            state[0] = jnp.zeros((dv, dk), F32)
+            out_a[...] = mm(xbuf[0, 0:tile], wall[:, start : start + group], NN)
+            out_b[...] = mm(xbuf[0, tile : 2 * tile], wall[:, start : start + group], NN)
+            rate = r_recv[j, 0:1, :]
+            post(out_a, 0, other, rate, None, dout_at, None)
+            post(out_b, 1, other, rate, None, dout_at, None)
+
+        def run(i, carry):
+            rows = pl.ds(pl.multiple_of(i * CH, CH), CH)
+            found = grads(i, other, r_recv[j, 0:1, :], dout_at, True)
+            for (lo, hi), grad in zip(bounds, found):
+                gmat[rows, slots[j] * group + lo : slots[j] * group + hi] = grad.astype(BF16)
+            return carry
+
+        def after():
+            for n in range(2):
+                copy_st(j, n).wait_recv()
+            edge[0] = st_recv[j, 0]
+            edge[1] = st_recv[j, 1]
+            enter_leave(other, each)
+            lax.fori_loop(0, each, run, 0)
+
+        return before, after
+
+    def arrived(j):
         copy_r(j).wait_recv()
         copy_d(j).wait_recv()
-        for n in range(2):
-            copy_st(j, n).wait_recv()
-        rate = r_recv[j, 0:1, :]
-
-        def dout_at(rows):
-            return d_recv[j, rows, :].astype(BF16)
-
-        state[0] = st_recv[j, 0]
-        edge[1] = st_recv[j, 1]
-        out_a[...] = mm(xbuf[0, 0:tile], wall[:, start : start + group], NN)
-        out_b[...] = mm(xbuf[0, tile : 2 * tile], wall[:, start : start + group], NN)
-        post(out_a, 0, rate, None, dout_at, None)
-        post(out_b, 1, rate, None, dout_at, None)
-        leave_from(each)
-
-        def run(i, carry):
-            rows = pl.ds(pl.multiple_of(i * CH, CH), CH)
-            for (lo, hi), grad in zip(bounds, grads(i, rate, dout_at, True)):
-                gmat[rows, (j + 1) * group + lo : (j + 1) * group + hi] = grad.astype(BF16)
+
+    def scatter(d):
+        to = lax.rem(me + d, seq)
+        return remote(msg.at[to], got.at[d], e1_s.at[d], e1_r.at[d], "seq", to)
+
+    def collect(d):
+        to = lax.rem(me + d, seq)
+        return remote(rep.at[to], back.at[me], e2_s.at[d], e2_r.at[d], "seq", to)
+
+    def start_all(copy):
+        def run(d, carry):
+            copy(d).start()
             return carry
 
-        lax.fori_loop(0, each, run, 0)
-
-    near(0)
-    pump(PUMP_NEAR)
-    near(1)
-
-    step = 512 if width % 512 == 0 else width
+        lax.fori_loop(1, seq, run, 0)
+
+    def wait_all(copy):
+        def run(d, carry):
+            copy(d).wait()
+            return carry
+
+        lax.fori_loop(1, seq, run, 0)
+
+    def fold_states(p, run):
+        it = lax.rem(me + seq - p, seq)
+        rep[p, 0:part, :] = run
+        return got[it, pl.ds(2 * part, 1), :] * run + got[it, pl.ds(0, part), :]
+
+    def fold_grads(n, run):
+        p = seq - 1 - n
+        it = lax.rem(me + seq - p, seq)
+        rep[p, part:, :] = run
+        return got[it, pl.ds(2 * part, 1), :] * run + got[it, pl.ds(part, part), :]
+
+    def scatter_start():
+        start_all(scatter)
+        got[0] = msg[me]
+
+    def fold():
+        wait_all(scatter)
+        lax.fori_loop(0, seq, fold_states, jnp.zeros((part, dk), F32))
+        lax.fori_loop(0, seq, fold_grads, jnp.zeros((part, dk), F32))
+        start_all(collect)
+        back[me] = rep[me]
+
+    def own_states():
+        wait_all(collect)
+        edge[0] = back[:, 0:part, :].reshape(dv, dk)
+        edge[1] = back[:, part:, :].reshape(dv, dk)
+        enter_leave(own, blocks)
+        for j in range(3):
+            copy_st(j, 0).start()
+            copy_st(j, 1).start()
+
+    def signal_of(b, pre):
+        sig_ref[pl.ds(pl.multiple_of(b * CH, CH), CH), :] = pre * scale
+
+    def home(i, carry):
+        b = rank * each + i
+        found = grads(b, own, own_rate, own_dout, True)
+        signal_of(b, found[3])
+        rows = pl.ds(pl.multiple_of(i * CH, CH), CH)
+        for (lo, hi), grad in zip(bounds, found):
+            gmat[rows, lo:hi] = grad.astype(BF16)
+        return carry
+
+    def aside(i, carry):
+        for j in range(3):
+            b = target[j] * each + i
+            signal_of(b, grads(b, own, own_rate, own_dout, False))
+        return carry
 
     def gather_own(n, carry):
         cols = pl.ds(pl.multiple_of(n * step, step), step)
         acc[n] = mm(gmat[...], wall[cols, :], NT)
         return carry
 
-    lax.fori_loop(0, width // step, gather_own, 0)
-    for event in events:
-        gather(*event)
-    unpack(2)
-    for i in range(each):
-        copy_g(i).wait_recv()
-        gmat[i * CH : (i + 1) * CH, 0:group] = g_recv[i].astype(BF16)
-    start = slots[2] * group
+    def signals_out():
+        for i in range(tp):
+            copy_sig(i).start()
+
+    def own_chunk():
+        x_copy(rank, 0).wait()
+
+    heads = [near(j) for j in range(3)]
+    steps = {
+        "scatter": scatter_start, "fold": fold, "states": own_states, "chunk": own_chunk,
+        "signals": signals_out,
+        "home": lambda lo, hi: lax.fori_loop(lo, hi, home, 0),
+        "aside": lambda lo, hi: lax.fori_loop(lo, hi, aside, 0),
+        "before": lambda j: (arrived(j), heads[j][0]()),
+        "after": lambda j: heads[j][1](),
+        "backproject": lambda: lax.fori_loop(0, width // step, gather_own, 0),
+        "gather": gather,
+    }
+    for name, *args in PLAN:
+        steps[name](*args)
+    at = slots[2] * group
     for n in range(width // step):
         cols = slice(n * step, (n + 1) * step)
         grad_ref[:, cols] = (
-            acc[n] + mm(gmat[:, 0:group], wall[cols, start : start + group], NT)
+            acc[n] + mm(gmat[:, at : at + group], wall[cols, at : at + group], NT)
         ).astype(BF16)
+        copy_grad(n).start()
 
     for j in range(3):
         w_cross(j).wait_send()
+        copy_r(j).wait_send()
+        copy_d(j).wait_send()
+        for n in range(2):
+            copy_st(j, n).wait_send()
         for n in range(4):
             w_line(j, n).wait_send()
             w_pair(j, n).wait_send()
         for n in range(12):
             w_plane(j, n).wait_send()
-    for j in range(2):
-        copy_r(j).wait_send()
-        copy_d(j).wait_send()
-    for i in range(each):
-        copy_g(i).wait_send()
-
-
-EVENTS = (
-    (0, 0), (1, 0), (2, 0), (0, 1), (1, 1), (2, 1), (0, 2), (1, 2), (2, 2),
-    (0, 3), (0, 4), (1, 3), (1, 4), (2, 3), (2, 4),
+    for i in range(tp):
+        copy_sig(i).wait()
+    for n in range(width // step):
+        copy_grad(n).wait()
+
+
+EARLY = ((2, 0, 0), (3, 1, 0))
+PLAN = (
+    ("scatter",), ("gather", 0, 1), ("gather", 0, 7), ("gather", 1, 7), ("gather", 2, 6),
+    ("gather", 0, 2), ("fold",),
+    ("gather", 0, 3), ("gather", 0, 4), ("gather", 1, 1), ("gather", 2, 7), ("chunk",),
+    ("gather", 1, 2), ("gather", 1, 3), ("gather", 2, 0), ("gather", 0, 5),
+    ("before", 0), ("gather", 1, 4), ("gather", 2, 1), ("states",),
+    ("home", 0, 2), ("gather", 1, 5), ("home", 2, 4), ("gather", 2, 2),
+    ("after", 0), ("gather", 2, 3), ("before", 1), ("gather", 2, 4), ("after", 1),
+    ("aside", 0, 2), ("gather", 2, 5), ("aside", 2, 4), ("signals",),
+    ("backproject",), ("before", 2), ("after", 2),
 )
-PUMPS_PROJECT = (0, 0, 2, 0)
-PUMP_SCATTER = 3
-PUMP_COLLECT = 3
-PUMPS_AWAY = (0, 0, 1, 1)
-PUMPS_HOME = (0, 0, 0, 1)
-PUMPS_ASIDE = (0, 0, 0, 1)
-PUMP_NEAR = 2
 
 
 def solution(mesh):
@@ -533,19 +542,28 @@
                 jax.ShapeDtypeStruct((chunk, width), BF16),
                 jax.ShapeDtypeStruct((length, dk), F32),
             ),
-            in_specs=[hbm] * 5 + [vmem] * 2,
-            out_specs=(vmem, vmem),
+            in_specs=[hbm] * 5 + [vmem, hbm],
+            out_specs=(hbm, hbm),
             scratch_shapes=[
                 pltpu.VMEM((width, 3 * group), BF16),
                 pltpu.VMEM((2, 2 * tile, width), BF16),
                 pltpu.VMEM((tile, group), F32),
                 pltpu.VMEM((tile, group), F32),
+                pltpu.VMEM((length, dv), BF16),
+                pltpu.VMEM((length, dk), F32),
+                pltpu.VMEM((chunk, width), BF16),
                 pltpu.VMEM((length, 2 * dk + dv), BF16),
                 pltpu.VMEM((length, dk), F32),
                 pltpu.VMEM((length, dk), F32),
                 pltpu.VMEM((blocks, dv, dk), F32),
                 pltpu.VMEM((blocks, dv, dk), F32),
                 pltpu.VMEM((blocks, PAD, dk), F32),
+                pltpu.VMEM((chunk, 2 * dk + dv), BF16),
+                pltpu.VMEM((chunk, dk), F32),
+                pltpu.VMEM((chunk, dk), F32),
+                pltpu.VMEM((each, dv, dk), F32),
+                pltpu.VMEM((each, dv, dk), F32),
+                pltpu.VMEM((each, PAD, dk), F32),
                 pltpu.VMEM((2, dv, dk), F32),
                 pltpu.VMEM((seq, 2 * part + PAD, dk), F32),
                 pltpu.VMEM((seq, 2 * part + PAD, dk), F32),
@@ -555,25 +573,22 @@
                 pltpu.VMEM((depth, group), F32),
                 pltpu.VMEM((3, 4, 4, depth, group), F32),
                 pltpu.VMEM((3, 4, 4, depth, group), F32),
-                pltpu.VMEM((2, chunk, dv), F32),
-                pltpu.VMEM((2, chunk, dv), F32),
+                pltpu.VMEM((3, chunk, dv), F32),
+                pltpu.VMEM((3, chunk, dv), F32),
                 pltpu.VMEM((PAD, dk), F32),
-                pltpu.VMEM((2, PAD, dk), F32),
-                pltpu.VMEM((2, 2, dv, dk), F32),
-                pltpu.VMEM((each, CH, group), F32),
-                pltpu.VMEM((each, CH, group), F32),
+                pltpu.VMEM((3, PAD, dk), F32),
+                pltpu.VMEM((3, 2, dv, dk), F32),
                 pltpu.VMEM((chunk, 3 * group), BF16),
                 pltpu.VMEM((width // step, chunk, step), F32),
             ]
-            + [dma((4,)), dma((2,))]
+            + [dma((5,)), dma((2,)), dma((tp + width // step,))]
             + [dma((seq,))] * 4
             + [dma((3,))] * 2
             + [dma((3, 4))] * 2
             + [dma((3, 12))] * 2
             + [dma((3, 4))] * 2
-            + [dma((2,))] * 4
-            + [dma((2, 2))] * 2
-            + [dma((each,))] * 2
+            + [dma((3,))] * 4
+            + [dma((3, 2))] * 2
             + [pltpu.SemaphoreType.REGULAR((2,))],
             compiler_params=pltpu.CompilerParams(
                 collective_id=0, has_side_effects=True, vmem_limit_bytes=VMEM_LIMIT

time: 125 us -> 102 us (0.82)
  Pallas kernels: 120 us -> 95.6 us
    pallas_call x1, Pallas kernels: 120 us -> 95.6 us  [body(): pl.pallas_call(functools.partial(kernel, seq, tp, dk, dv, tile, scale), o...]
where the time goes in v3:
time: 102 us; the launch traced here: 101 us
  Pallas kernels  95.6 us (94%)
  local copies, waits for them, and re-layouts  4.46 us (4%)
    pallas_call x1, Pallas kernels, body(): pl.pallas_call(functools.partial(kernel, seq, tp, dk, dv, tile, scale), o...  95.6 us
    unnamed x4, local copies, waits for them, and re-layouts  4.46 us

profile of v3, /device:TPU:1, one launch (start us, length us, event | category | flops | bytes accessed | tf_op | source)
XLA Modules:
  0.0 100.7 jit_solution(2830040097963981427)
XLA Ops:
  0.6 95.6 %shard_map.86 = (bf16[512,2560]{1,0:T(8,128)(2,1)}, f32[2048,128]{1,0:T(8,128)}) custom-call(bf16[2048,2560]{1,0:T(8,128)(2,1)} %tok.1, bf16[2560,128]{1,0:T(8,128)(2,1)} %wq.1, bf16[2560,128]{1,0:T(8,128)(2,1)} %wk.1, bf16[2560,256]{1,0:T(8,128)(2,1)} %wv.1, bf16[2560,128]{1,0:T(8,128)(2,1)} %wg.1, f32[1,128]{1,0:T(1,128)} %bitcast.1, bf16[2048,256]{1,0:T(8,128)(2,1)} %dout_in.1), custom_call_target="tpu_custom_call" | custom-call | tf_op jit(solution)/shard_map/pallas_call | solution.py:539
  96.2 0.0 copy-start
  96.2 3.5 %copy.11 = bf16[512,2560]{1,0:T(8,128)(2,1)} copy(bf16[512,2560]{1,0:T(8,128)(2,1)} %get-tuple-element.4) | data formatting | bytes 5242880
  99.7 0.0 copy-done
  99.7 1.0 copy.12
Async XLA Ops:
  96.2 3.5 %copy-start = (f32[2048,128]{1,0:T(8,128)S(1)}, f32[2048,128]{1,0:T(8,128)}, u32[]{:S(2)}) copy-start(f32[2048,128]{1,0:T(8,128)} %get-tuple-element.5) | copy-start | bytes 3145732

commit v4 on v3

--- a/solution.py
+++ b/solution.py
@@ -10,7 +10,7 @@
 
 CH = 128
 PAD = 8
-VMEM_LIMIT = 67_043_328
+VMEM_LIMIT = 63_200_000
 F32, BF16 = jnp.float32, jnp.bfloat16
 
 
@@ -32,11 +32,11 @@
 def kernel(
     seq, tp, dk, dv, tile, scale,
     tok, wq, wk, wv, wg, rate_ref, dout_in,
-    grad_out, sig_out,
-    wall, xbuf, out_a, out_b, dout_ref, sig_ref, grad_ref, proj, sq_all, w_all, s_all, m_all, cl_all,
+    grad_ref, sig_ref,
+    wall, xbuf, out_a, out_b, dout_ref, proj, sq_all, w_all, s_all, m_all, cl_all,
     proj_n, sq_n, w_n, s_n, m_n, cl_n, state, msg, got, rep, back, edge,
-    wown, land, landd, d_send, d_recv, r_send, r_recv, st_recv, gmat, acc,
-    w_sem, x_sem, o_sem, e1_s, e1_r, e2_s, e2_r, y_s, y_r, p1_s, p1_r, p2_s, p2_r, dd_s, dd_r,
+    wown, wmore, land, landd, d_send, d_recv, r_send, r_recv, st_recv, gmat, acc,
+    w_sem, x_sem, e1_s, e1_r, e2_s, e2_r, y_s, y_r, ym_s, ym_r, p1_s, p1_r, p2_s, p2_r, dd_s, dd_r,
     do_s, do_r, ra_s, ra_r, st_s, st_r, met,
 ):
     me, rank = lax.axis_index("seq"), lax.axis_index("tp")
@@ -80,6 +80,12 @@
 
     def w_cross(j):
         return remote(wown, land.at[j, 0, 0], y_s.at[j], y_r.at[j], "tp", target[j])
+
+    def w_more(j, n):
+        a = 3 * n
+        return remote(
+            wmore.at[n], land.at[j, 2, a], ym_s.at[j, n], ym_r.at[j, n], "tp", target[j]
+        )
 
     def w_line(j, n):
         half = depth // 2
@@ -134,7 +140,8 @@
             for a in (0, 3):
                 w_plane(j, a).wait_recv()
                 w_plane(j, 4 + a).wait_recv()
-                w_plane(j, 8 + a).start()
+                if j == 2:
+                    w_plane(j, 8 + a).start()
         elif stage == 4:
             for a in (1, 2):
                 w_plane(j, a).wait_recv()
@@ -143,9 +150,16 @@
             w_pair(j, 3).start()
             w_pair(j, 1).start()
         elif stage == 5:
-            for a in range(4):
-                w_plane(j, 8 + a).wait_recv()
+            for n in range(2):
+                if j == 2:
+                    w_plane(j, 8 + 3 * n).wait_recv()
+                else:
+                    w_more(j, n).wait_recv()
+                w_plane(j, 9 + n).wait_recv()
             w_pair(j, 2).start()
+        elif stage == 8:
+            w_more(j, 0).start()
+            w_more(j, 1).start()
         elif stage == 6:
             w_cross(j).start()
         else:
@@ -166,14 +180,6 @@
     def copy_st(j, n):
         source = (s_all.at[target[j] * each], m_all.at[target[j] * each + each - 1])[n]
         return remote(source, st_recv.at[j, n], st_s.at[j, n], st_r.at[j, n], "tp", target[j])
-
-    def copy_sig(i):
-        rows = pl.ds(pl.multiple_of(i * chunk, chunk), chunk)
-        return pltpu.make_async_copy(sig_ref.at[rows], sig_out.at[rows], o_sem.at[i])
-
-    def copy_grad(n):
-        cols = pl.ds(n * step, step)
-        return pltpu.make_async_copy(grad_ref.at[:, cols], grad_out.at[:, cols], o_sem.at[tp + n])
 
     loads = []
     for n, (w, start, size) in enumerate(
@@ -206,6 +212,10 @@
     r_send[...] = jnp.broadcast_to(own_rate, (PAD, dk))
     for load in loads:
         load.wait()
+    for n in range(2):
+        origin = seq_at(3 * n * (1 - core) + 2 * core, 3 * n * core + 2 * (1 - core), core)
+        rows = pl.ds(pl.multiple_of(origin * depth, 16), depth)
+        wmore[n] = wall[rows, 0:group].astype(F32)
     wown[...] = wall[pl.ds(pl.multiple_of(me * depth, 16), depth), 0:group].astype(F32)
     pl.semaphore_wait(barrier, 2 * side - 1 + tp - 1)
     for j in range(2):
@@ -218,6 +228,14 @@
     for j in range(3):
         rows = pl.ds(pl.multiple_of(target[j] * chunk, chunk), chunk)
         d_send[j] = dout_ref[rows, :].astype(F32)
+
+    def project_rows(out, slot, at, start):
+        rows, half = slice(at, at + tile), width // 2
+        cut = start + 2 * dk + dv
+        out[:, : 2 * dk + dv] = mm(xbuf[slot, rows], wall[:, start:cut], NN)
+        out[:, 2 * dk + dv :] = mm(
+            xbuf[slot, rows, :half], wall[:half, cut : start + group], NN
+        ) + mm(xbuf[slot, rows, half:], wall[half:, cut : start + group], NN)
 
     def post(out, t, kept, rate, total, dout_at, slope):
         proj, sq_all, w_all, s_all, m_all, cl_all = kept
@@ -264,12 +282,12 @@
             def _():
                 gather(*event)
 
-        out_a[...] = mm(xbuf[slot, 0:tile], wall[:, 0:group], NN)
+        project_rows(out_a, slot, 0, 0)
         total = post(
             out_b, jnp.maximum(2 * k - 1, 0), own, own_rate, total, own_dout,
             jnp.minimum(k, 1).astype(F32),
         )
-        out_b[...] = mm(xbuf[slot, tile : 2 * tile], wall[:, 0:group], NN)
+        project_rows(out_b, slot, tile, 0)
         return post(out_a, 2 * k, own, own_rate, total, own_dout, 1.0)
 
     total = lax.fori_loop(0, pairs, project, jnp.zeros((1, dk), F32))
@@ -335,20 +353,18 @@
 
     bounds = ((0, dk), (dk, 2 * dk), (2 * dk, 2 * dk + dv), (2 * dk + dv, group))
 
-    def unpack(j):
+    def unpack(j, b):
         start = slots[j] * group
-        for b in range(4):
-            w_pair(j, b).wait_recv()
-
-        def run(n, carry):
-            b, a = n // 4, lax.rem(n, 4)
+        w_pair(j, b).wait_recv()
+
+        def run(a, carry):
             for buffer, on in ((land, core), (landd, 1 - core)):
                 origin = seq_at(a * (1 - on) + b * on, a * on + b * (1 - on), on)
                 rows = pl.ds(pl.multiple_of(origin * depth, 16), depth)
                 wall[rows, start : start + group] = buffer[j, b, a].astype(BF16)
             return carry
 
-        lax.fori_loop(0, 16, run, 0)
+        lax.fori_loop(0, 4, run, 0)
 
     def near(j):
         start = slots[j] * group
@@ -356,19 +372,20 @@
             return d_recv[j, rows, :].astype(BF16)
 
         def before():
-            unpack(j)
             state[0] = jnp.zeros((dv, dk), F32)
-            out_a[...] = mm(xbuf[0, 0:tile], wall[:, start : start + group], NN)
-            out_b[...] = mm(xbuf[0, tile : 2 * tile], wall[:, start : start + group], NN)
+            project_rows(out_a, 0, 0, start)
+            project_rows(out_b, 0, tile, start)
             rate = r_recv[j, 0:1, :]
             post(out_a, 0, other, rate, None, dout_at, None)
             post(out_b, 1, other, rate, None, dout_at, None)
 
-        def run(i, carry):
-            rows = pl.ds(pl.multiple_of(i * CH, CH), CH)
-            found = grads(i, other, r_recv[j, 0:1, :], dout_at, True)
-            for (lo, hi), grad in zip(bounds, found):
-                gmat[rows, slots[j] * group + lo : slots[j] * group + hi] = grad.astype(BF16)
+        def run(h, carry):
+            rate = r_recv[j, 0:1, :]
+            pair = [grads(2 * h + n, other, rate, dout_at, True) for n in range(2)]
+            for n in range(2):
+                rows = pl.ds(pl.multiple_of((2 * h + n) * CH, CH), CH)
+                for (lo, hi), grad in zip(bounds, pair[n]):
+                    gmat[rows, slots[j] * group + lo : slots[j] * group + hi] = grad.astype(BF16)
             return carry
 
         def after():
@@ -377,7 +394,7 @@
             edge[0] = st_recv[j, 0]
             edge[1] = st_recv[j, 1]
             enter_leave(other, each)
-            lax.fori_loop(0, each, run, 0)
+            lax.fori_loop(0, each // 2, run, 0)
 
         return before, after
 
@@ -441,29 +458,31 @@
     def signal_of(b, pre):
         sig_ref[pl.ds(pl.multiple_of(b * CH, CH), CH), :] = pre * scale
 
-    def home(i, carry):
-        b = rank * each + i
-        found = grads(b, own, own_rate, own_dout, True)
-        signal_of(b, found[3])
-        rows = pl.ds(pl.multiple_of(i * CH, CH), CH)
-        for (lo, hi), grad in zip(bounds, found):
-            gmat[rows, lo:hi] = grad.astype(BF16)
+    def home(h, carry):
+        pair = [grads(rank * each + 2 * h + n, own, own_rate, own_dout, True) for n in range(2)]
+        for n in range(2):
+            i = 2 * h + n
+            signal_of(rank * each + i, pair[n][3])
+            rows = pl.ds(pl.multiple_of(i * CH, CH), CH)
+            for (lo, hi), grad in zip(bounds, pair[n]):
+                gmat[rows, lo:hi] = grad.astype(BF16)
         return carry
 
     def aside(i, carry):
+        found = [grads(target[j] * each + i, own, own_rate, own_dout, False) for j in range(3)]
         for j in range(3):
-            b = target[j] * each + i
-            signal_of(b, grads(b, own, own_rate, own_dout, False))
+            signal_of(target[j] * each + i, found[j])
         return carry
 
-    def gather_own(n, carry):
-        cols = pl.ds(pl.multiple_of(n * step, step), step)
-        acc[n] = mm(gmat[...], wall[cols, :], NT)
-        return carry
-
-    def signals_out():
-        for i in range(tp):
-            copy_sig(i).start()
+    def back_first(lo, hi):
+        for n in range(lo, hi):
+            cols = slice(n * step, (n + 1) * step)
+            acc[n] = mm(gmat[:, 0 : 2 * group], wall[cols, 0 : 2 * group], NT)
+
+    def back_next(lo, hi):
+        for n in range(lo, hi):
+            cols = slice(n * step, (n + 1) * step)
+            acc[n] += mm(gmat[:, 2 * group :], wall[cols, 2 * group :], NT)
 
     def own_chunk():
         x_copy(rank, 0).wait()
@@ -471,13 +490,12 @@
     heads = [near(j) for j in range(3)]
     steps = {
         "scatter": scatter_start, "fold": fold, "states": own_states, "chunk": own_chunk,
-        "signals": signals_out,
         "home": lambda lo, hi: lax.fori_loop(lo, hi, home, 0),
         "aside": lambda lo, hi: lax.fori_loop(lo, hi, aside, 0),
         "before": lambda j: (arrived(j), heads[j][0]()),
         "after": lambda j: heads[j][1](),
-        "backproject": lambda: lax.fori_loop(0, width // step, gather_own, 0),
-        "gather": gather,
+        "back_first": back_first, "back_next": back_next,
+        "gather": gather, "unpack": unpack,
     }
     for name, *args in PLAN:
         steps[name](*args)
@@ -487,7 +505,6 @@
         grad_ref[:, cols] = (
             acc[n] + mm(gmat[:, at : at + group], wall[cols, at : at + group], NT)
         ).astype(BF16)
-        copy_grad(n).start()
 
     for j in range(3):
         w_cross(j).wait_send()
@@ -499,24 +516,28 @@
             w_line(j, n).wait_send()
             w_pair(j, n).wait_send()
         for n in range(12):
-            w_plane(j, n).wait_send()
-    for i in range(tp):
-        copy_sig(i).wait()
-    for n in range(width // step):
-        copy_grad(n).wait()
-
-
-EARLY = ((2, 0, 0), (3, 1, 0))
+            if j == 2 or n not in (8, 11):
+                w_plane(j, n).wait_send()
+        if j < 2:
+            w_more(j, 0).wait_send()
+            w_more(j, 1).wait_send()
+
+
+EARLY = ((2, 0, 0), (2, 2, 6), (3, 1, 0), (3, 0, 8), (3, 1, 8))
 PLAN = (
-    ("scatter",), ("gather", 0, 1), ("gather", 0, 7), ("gather", 1, 7), ("gather", 2, 6),
-    ("gather", 0, 2), ("fold",),
-    ("gather", 0, 3), ("gather", 0, 4), ("gather", 1, 1), ("gather", 2, 7), ("chunk",),
-    ("gather", 1, 2), ("gather", 1, 3), ("gather", 2, 0), ("gather", 0, 5),
-    ("before", 0), ("gather", 1, 4), ("gather", 2, 1), ("states",),
-    ("home", 0, 2), ("gather", 1, 5), ("home", 2, 4), ("gather", 2, 2),
-    ("after", 0), ("gather", 2, 3), ("before", 1), ("gather", 2, 4), ("after", 1),
-    ("aside", 0, 2), ("gather", 2, 5), ("aside", 2, 4), ("signals",),
-    ("backproject",), ("before", 2), ("after", 2),
+    ("scatter",), ("gather", 0, 1), ("gather", 0, 2), ("gather", 0, 7), ("gather", 1, 7),
+    ("fold",), ("gather", 0, 3), ("gather", 0, 4), ("gather", 1, 1),
+    ("chunk",), ("unpack", 0, 0),
+    ("gather", 1, 2), ("states",), ("gather", 2, 7), ("home", 0, 1), ("gather", 1, 3),
+    ("home", 1, 2), ("gather", 0, 5), ("gather", 2, 0),
+    ("unpack", 0, 3), ("unpack", 0, 1), ("gather", 1, 4), ("unpack", 0, 2),
+    ("before", 0), ("aside", 0, 1), ("gather", 2, 1), ("unpack", 1, 0), ("aside", 1, 2),
+    ("gather", 1, 5), ("unpack", 1, 3), ("gather", 2, 2),
+    ("after", 0), ("gather", 2, 3), ("unpack", 1, 1), ("unpack", 1, 2),
+    ("before", 1), ("gather", 2, 4), ("after", 1), ("back_first", 0, 5), ("gather", 2, 5),
+    ("back_next", 0, 5), ("aside", 2, 4),
+    ("unpack", 2, 0), ("unpack", 2, 3), ("unpack", 2, 1), ("unpack", 2, 2),
+    ("before", 2), ("after", 2),
 )
 
 
@@ -539,19 +560,17 @@
         return pl.pallas_call(
             functools.partial(kernel, seq, tp, dk, dv, tile, scale),
             out_shape=(
-                jax.ShapeDtypeStruct((chunk, width), BF16),
-                jax.ShapeDtypeStruct((length, dk), F32),
+                pltpu.VMEM((chunk, width), BF16),
+                pltpu.VMEM((length, dk), F32),
             ),
             in_specs=[hbm] * 5 + [vmem, hbm],
-            out_specs=(hbm, hbm),
+            out_specs=(vmem, vmem),
             scratch_shapes=[
                 pltpu.VMEM((width, 3 * group), BF16),
                 pltpu.VMEM((2, 2 * tile, width), BF16),
                 pltpu.VMEM((tile, group), F32),
                 pltpu.VMEM((tile, group), F32),
                 pltpu.VMEM((length, dv), BF16),
-                pltpu.VMEM((length, dk), F32),
-                pltpu.VMEM((chunk, width), BF16),
                 pltpu.VMEM((length, 2 * dk + dv), BF16),
                 pltpu.VMEM((length, dk), F32),
                 pltpu.VMEM((length, dk), F32),
@@ -571,6 +590,7 @@
                 pltpu.VMEM((seq, 2 * part, dk), F32),
                 pltpu.VMEM((2, dv, dk), F32),
                 pltpu.VMEM((depth, group), F32),
+                pltpu.VMEM((2, depth, group), F32),
                 pltpu.VMEM((3, 4, 4, depth, group), F32),
                 pltpu.VMEM((3, 4, 4, depth, group), F32),
                 pltpu.VMEM((3, chunk, dv), F32),
@@ -581,9 +601,10 @@
                 pltpu.VMEM((chunk, 3 * group), BF16),
                 pltpu.VMEM((width // step, chunk, step), F32),
             ]
-            + [dma((5,)), dma((2,)), dma((tp + width // step,))]
+            + [dma((5,)), dma((2,))]
             + [dma((seq,))] * 4
             + [dma((3,))] * 2
+            + [dma((2, 2))] * 2
             + [dma((3, 4))] * 2
             + [dma((3, 12))] * 2
             + [dma((3, 4))] * 2

time: 102 us -> 91.6 us (0.90)
  Pallas kernels: 95.6 us -> 87 us
  local copies, waits for them, and re-layouts: 4.46 us -> 2.46 us
    pallas_call x1, Pallas kernels: 95.6 us -> 87 us  [body(): pl.pallas_call(functools.partial(kernel, seq, tp, dk, dv, tile, scale), o...]
    unnamed x4 -> x2, local copies, waits for them, and re-layouts: 4.46 us -> 2.46 us
where the time goes in v4:
time: 91.6 us; the launch traced here: 90.1 us
  Pallas kernels  87 us (95%)
  local copies, waits for them, and re-layouts  2.46 us (3%)
    pallas_call x1, Pallas kernels, body(): pl.pallas_call(functools.partial(kernel, seq, tp, dk, dv, tile, scale), o...  87 us
    unnamed x2, local copies, waits for them, and re-layouts  2.46 us

profile of v4, /device:TPU:1, one launch (start us, length us, event | category | flops | bytes accessed | tf_op | source)
XLA Modules:
  0.0 90.1 jit_solution(4075447777394846837)
XLA Ops:
  0.6 87.0 %shard_map.86 = (bf16[512,2560]{1,0:T(8,128)(2,1)S(1)}, f32[2048,128]{1,0:T(8,128)S(1)}) custom-call(bf16[2048,2560]{1,0:T(8,128)(2,1)} %tok.1, bf16[2560,128]{1,0:T(8,128)(2,1)} %wq.1, bf16[2560,128]{1,0:T(8,128)(2,1)} %wk.1, bf16[2560,256]{1,0:T(8,128)(2,1)} %wv.1, bf16[2560,128]{1,0:T(8,128)(2,1)} %wg.1, f32[1,128]{1,0:T(1,128)} %bitcast.1, ...), custom_call_target="tpu_custom_call" | custom-call | tf_op jit(solution)/shard_map/pallas_call | solution.py:560
  87.6 1.5 %copy.11 = bf16[512,2560]{1,0:T(8,128)(2,1)} copy(bf16[512,2560]{1,0:T(8,128)(2,1)S(1)} %get-tuple-element.2) | data formatting | bytes 5242880
  89.1 1.0 %copy.12 = f32[2048,128]{1,0:T(8,128)} copy(f32[2048,128]{1,0:T(8,128)S(1)} %get-tuple-element.3) | data formatting | bytes 2097152

commit v5 on v4

--- a/solution.py
+++ b/solution.py
@@ -298,7 +298,7 @@
 
     msg[:, 0:part, :] = state[0].reshape(seq, part, dk)
     msg[:, part : 2 * part, :] = state[1].reshape(seq, part, dk)
-    msg[:, 2 * part :, :] = jnp.broadcast_to(jnp.exp(total)[None], (seq, PAD, dk))
+    msg[:, 2 * part :, :] = jnp.broadcast_to(jnp.exp(total)[None], (seq, 1, dk))
     pl.semaphore_wait(met.at[1], 1)
 
     def enter_leave(kept, count):
@@ -451,7 +451,7 @@
         edge[0] = back[:, 0:part, :].reshape(dv, dk)
         edge[1] = back[:, part:, :].reshape(dv, dk)
         enter_leave(own, blocks)
-        for j in range(3):
+        for j in range(2):
             copy_st(j, 0).start()
             copy_st(j, 1).start()
 
@@ -484,6 +484,11 @@
             cols = slice(n * step, (n + 1) * step)
             acc[n] += mm(gmat[:, 2 * group :], wall[cols, 2 * group :], NT)
 
+    def far_start():
+        copy_st(2, 0).start()
+        copy_st(2, 1).start()
+        copy_d(2).start()
+
     def own_chunk():
         x_copy(rank, 0).wait()
 
@@ -495,7 +500,7 @@
         "before": lambda j: (arrived(j), heads[j][0]()),
         "after": lambda j: heads[j][1](),
         "back_first": back_first, "back_next": back_next,
-        "gather": gather, "unpack": unpack,
+        "gather": gather, "unpack": unpack, "far": far_start,
     }
     for name, *args in PLAN:
         steps[name](*args)
@@ -528,15 +533,14 @@
     ("scatter",), ("gather", 0, 1), ("gather", 0, 2), ("gather", 0, 7), ("gather", 1, 7),
     ("fold",), ("gather", 0, 3), ("gather", 0, 4), ("gather", 1, 1),
     ("chunk",), ("unpack", 0, 0),
-    ("gather", 1, 2), ("states",), ("gather", 2, 7), ("home", 0, 1), ("gather", 1, 3),
-    ("home", 1, 2), ("gather", 0, 5), ("gather", 2, 0),
-    ("unpack", 0, 3), ("unpack", 0, 1), ("gather", 1, 4), ("unpack", 0, 2),
-    ("before", 0), ("aside", 0, 1), ("gather", 2, 1), ("unpack", 1, 0), ("aside", 1, 2),
-    ("gather", 1, 5), ("unpack", 1, 3), ("gather", 2, 2),
-    ("after", 0), ("gather", 2, 3), ("unpack", 1, 1), ("unpack", 1, 2),
-    ("before", 1), ("gather", 2, 4), ("after", 1), ("back_first", 0, 5), ("gather", 2, 5),
-    ("back_next", 0, 5), ("aside", 2, 4),
-    ("unpack", 2, 0), ("unpack", 2, 3), ("unpack", 2, 1), ("unpack", 2, 2),
+    ("gather", 1, 2), ("states",), ("home", 0, 1), ("gather", 1, 3),
+    ("home", 1, 2), ("aside", 0, 1), ("gather", 0, 5), ("gather", 2, 0),
+    ("unpack", 0, 3), ("unpack", 0, 1), ("aside", 1, 2), ("gather", 1, 4), ("unpack", 0, 2),
+    ("before", 0), ("gather", 2, 1), ("far",), ("aside", 2, 3), ("unpack", 1, 0),
+    ("gather", 1, 5), ("unpack", 1, 3), ("unpack", 1, 1), ("gather", 2, 2), ("after", 0),
+    ("unpack", 1, 2), ("gather", 2, 3), ("before", 1), ("gather", 2, 4), ("after", 1),
+    ("back_first", 0, 5), ("gather", 2, 5), ("back_next", 0, 5),
+    ("unpack", 2, 0), ("unpack", 2, 3), ("unpack", 2, 1), ("aside", 3, 4), ("unpack", 2, 2),
     ("before", 2), ("after", 2),
 )
 
@@ -584,8 +588,8 @@
                 pltpu.VMEM((each, dv, dk), F32),
                 pltpu.VMEM((each, PAD, dk), F32),
                 pltpu.VMEM((2, dv, dk), F32),
-                pltpu.VMEM((seq, 2 * part + PAD, dk), F32),
-                pltpu.VMEM((seq, 2 * part + PAD, dk), F32),
+                pltpu.VMEM((seq, 2 * part + 1, dk), F32),
+                pltpu.VMEM((seq, 2 * part + 1, dk), F32),
                 pltpu.VMEM((seq, 2 * part, dk), F32),
                 pltpu.VMEM((seq, 2 * part, dk), F32),
                 pltpu.VMEM((2, dv, dk), F32),

time: 91.6 us -> 89.2 us (0.974); the launches traced: 90.1 us -> 88.7 us
  Pallas kernels: 87 us -> 85.6 us
    pallas_call x1, Pallas kernels: 87 us -> 85.6 us  [body(): pl.pallas_call(functools.partial(kernel, seq, tp, dk, dv, tile, scale), o...]
where the time goes in v5:
time: 89.2 us; the launch traced here: 88.7 us
  Pallas kernels  85.6 us (96%)
  local copies, waits for them, and re-layouts  2.46 us (3%)
    pallas_call x1, Pallas kernels, body(): pl.pallas_call(functools.partial(kernel, seq, tp, dk, dv, tile, scale), o...  85.6 us
    unnamed x2, local copies, waits for them, and re-layouts  2.46 us

profile of v5, /device:TPU:1, one launch (start us, length us, event | category | flops | bytes accessed | tf_op | source)
XLA Modules:
  0.0 88.7 jit_solution(15862531482022383083)
XLA Ops:
  0.6 85.6 %shard_map.86 = (bf16[512,2560]{1,0:T(8,128)(2,1)S(1)}, f32[2048,128]{1,0:T(8,128)S(1)}) custom-call(bf16[2048,2560]{1,0:T(8,128)(2,1)} %tok.1, bf16[2560,128]{1,0:T(8,128)(2,1)} %wq.1, bf16[2560,128]{1,0:T(8,128)(2,1)} %wk.1, bf16[2560,256]{1,0:T(8,128)(2,1)} %wv.1, bf16[2560,128]{1,0:T(8,128)(2,1)} %wg.1, f32[1,128]{1,0:T(1,128)} %bitcast.1, ...), custom_call_target="tpu_custom_call" | custom-call | tf_op jit(solution)/shard_map/pallas_call | solution.py:564
  86.2 1.5 %copy.11 = bf16[512,2560]{1,0:T(8,128)(2,1)} copy(bf16[512,2560]{1,0:T(8,128)(2,1)S(1)} %get-tuple-element.2) | data formatting | bytes 5242880
  87.7 1.0 %copy.12 = f32[2048,128]{1,0:T(8,128)} copy(f32[2048,128]{1,0:T(8,128)S(1)} %get-tuple-element.3) | data formatting | bytes 2097152
